TPU v7x, 128 devices: a whole 4x4x4 slice. The times are simulated.
128 devices in a mesh: tp: 2 (over core), dp: 64 (over z, y, x).
Axes of the slice: x: 4, y: 4, z: 4, core: 2. Of those that a mesh axis runs over, the one named last changes fastest.
Arguments:
- token_ids: int32 [1024, 512], P('dp')
- embed_table: bfloat16 [50304, 512], P('tp')
- ln1_gain: bfloat16 [512], replicated
- ln1_bias: bfloat16 [512], replicated
- ln2_gain: bfloat16 [512], replicated
- ln2_bias: bfloat16 [512], replicated
- w_qkv: bfloat16 [512, 8, 3, 64], P(None, 'tp')
- b_qkv: bfloat16 [8, 3, 64], P('tp')
- w_dense: bfloat16 [8, 64, 512], P('tp')
- b_dense: bfloat16 [512], replicated
- w_fc1: bfloat16 [512, 2048], P(None, 'tp')
- b_fc1: bfloat16 [2048], P('tp')
- w_fc2: bfloat16 [2048, 512], P('tp')
- b_fc2: bfloat16 [512], replicated
- cotangent: bfloat16 [1024, 512, 512], P('dp')
Outputs:
- output 1: bfloat16 [1024, 512, 512], P('dp')
- output 2: float32 [50304, 512], P('tp', 'dp')
- output 3: float32 [512], P('dp')
- output 4: float32 [512], P('dp')
- output 5: float32 [512], P('dp')
- output 6: float32 [512], P('dp')
- output 7: float32 [512, 8, 3, 64], P('dp', 'tp')
- output 8: float32 [1536], P(('tp', 'dp'))
- output 9: float32 [8, 64, 512], P('tp', None, 'dp')
- output 10: float32 [512], P('dp')
- output 11: float32 [512, 2048], P('dp', 'tp')
- output 12: float32 [2048], P(('tp', 'dp'))
- output 13: float32 [2048, 512], P('tp', 'dp')
- output 14: float32 [512], P('dp')
All inputs are finite; a program needn't handle non-finite values.
Results may differ from a plain program's by a relative error of at most 0.00955545.
Values sent between devices are 32-bit elements.
A program may use at most 1 GiB of HBM per device.

v0:
```python
import functools
import math
import jax
import jax.numpy as jnp
from jax import lax
from jax.experimental import pallas as pl
from jax.experimental.pallas import tpu as pltpu
from jax.sharding import PartitionSpec as P

F32, BF16 = jnp.float32, jnp.bfloat16
NN = (((1,), (0,)), ((), ()))
NT = (((1,), (1,)), ((), ()))
TN = (((0,), (0,)), ((), ()))
S, D, FF, HEADS, HD = 512, 512, 2048, 8, 64
PAIR, HALF, PAIRS, FF_STEPS, ROT_HALF = 2 * HD, S // 2, HEADS // 2, FF // S, HD // 8
EPS, ROPE_BASE = 1e-5, 10000.0
LOG2E = 1.4426950408889634
SQRT_HALF, INV_SQRT_2PI = 0.7071067811865476, 0.3989422804014327
RB = 128
VMEM_LIMIT = 67_000_000
ROW, LANES, RING = 8, 128, 4
PAD = 25600
COLOR = PAD // 2
PARTS = 2
WIDE, EXTRA = 3072, 128
GCOLS = WIDE + EXTRA
MESH = pl.DeviceIdType.MESH


def dot(a, b, dims=NN):
    return lax.dot_general(a, b, dims, preferred_element_type=F32)


def rnd(v):
    return v.astype(BF16).astype(F32)


def gelu_parts(a):
    phi = 0.5 + 0.5 * lax.erf(a * SQRT_HALF)
    return a * phi, phi + a * jnp.exp2(a * a * (-0.5 * LOG2E)) * INV_SQRT_2PI


def block(i, n):
    return slice(i * n, i * n + n)


def row_sums(v):
    return jnp.sum(v.reshape(v.shape[0] // ROW, ROW, v.shape[1]), axis=0)


def wcol(half, part, width):
    return slice(half * WIDE + part, half * WIDE + part + width)


def look_up_kernel(codes_ref, table_ref, peer_ref, own_ref, table, sem):
    step = pl.program_id(0)
    half = pl.num_programs(0) * S

    @pl.when(step == 0)
    def _():
        rows = table_ref.shape[0]
        load = pltpu.make_async_copy(table_ref, table.at[:rows], sem)
        load.start()
        table[rows:, :] = jnp.zeros((ROW, D), BF16)
        load.wait()
    sub = lax.broadcasted_iota(jnp.int32, (ROW, D), 0)

    def look_up(first):
        got = jnp.zeros((ROW, D), F32)
        for j in range(ROW):
            at = codes_ref[first + j]
            rows = table[pl.ds(pl.multiple_of(at & -ROW, ROW), ROW), :].astype(F32)
            got = jnp.where(sub == j, pltpu.roll(rows, (j - at) & (ROW - 1), 0), got)
        return got

    for k, dst in enumerate((own_ref, peer_ref)):
        @pl.loop(0, S // ROW, unroll=2)
        def _(g):
            t0 = pl.multiple_of(g * ROW, ROW)
            dst[0, pl.ds(t0, ROW), :] = look_up(k * half + step * S + t0).astype(dst.dtype)


def look_up_call(codes, table):
    seqs = codes.size // (2 * S)
    seq = pl.BlockSpec((1, S, D), lambda i, _: (i, 0, 0))
    return pl.pallas_call(
        look_up_kernel,
        grid_spec=pltpu.PrefetchScalarGridSpec(
            num_scalar_prefetch=1, grid=(seqs,), in_specs=[pl.BlockSpec(memory_space=pl.ANY)], out_specs=[seq] * 2,
            scratch_shapes=[pltpu.VMEM((table.shape[0] + ROW, D), BF16), pltpu.SemaphoreType.DMA]),
        out_shape=[jax.ShapeDtypeStruct((seqs, S, D), t) for t in (F32, BF16)],
        compiler_params=pltpu.CompilerParams(dimension_semantics=("arbitrary",), vmem_limit_bytes=VMEM_LIMIT),
        cost_estimate=pl.CostEstimate(flops=40_000_000_000, bytes_accessed=40_000_000, transcendentals=0),
        name="look_up",
    )(codes, table)


def layer_kernel(xo_ref, cot_ref, vec_ref, bo_ref, bp_ref, rope_ref, xs_ref, qo_ref, do_ref, fo_ref, to_ref, rp_ref, fp_ref,
                 out_ref, rows_ref, xin_ref, gw_out, gs_ref, gb1_ref,
                 gw_ref, wqkv, wd, w1, w2, n_scr, acc_scr, dh2_scr, dh1_scr, inv_scr, h1_scr, h2_scr, h1t_scr, h2t_scr, cott_scr, dctx_scr, ctx_scr,
                 qkv_scr, dqkv_scr, s_scr, dp_scr, pb_scr, ds_scr, a_scr, du_scr, u_scr, da_scr, dk_scr, dv_scr,
                 xp_buf, gx_buf, out_buf, peer_buf, own_low, peer_low, x_send, x_recv, x_load, gx_send, gx_recv, gx_local, out_send, out_recv, own_sem, peer_sem, init_sem):
    step, last = pl.program_id(0), pl.num_programs(0) - 1
    slot = step % 2
    core, chip = lax.axis_index('tp'), lax.axis_index('dp')
    chips = lax.axis_size('dp')
    plane = chips // RING
    z, peer = chip // plane, (1 - core, chip)

    def z_device(k):
        return (core, (chip + k * plane) % chips)

    def x_copy(at):
        return pltpu.make_async_remote_copy(xs_ref.at[at], xin_ref.at[at], x_send.at[at], x_recv.at[at], device_id=peer, device_id_type=MESH)

    def x_take(at):
        return pltpu.make_async_copy(xin_ref.at[at], xp_buf.at[at % 2], x_load.at[at % 2])

    @pl.when(step == 0)
    def _():
        barrier = pltpu.get_barrier_semaphore()
        near = [peer] + [z_device(k) for k in range(1, RING)]
        for who in near:
            pl.semaphore_signal(barrier, inc=1, device_id=who, device_id_type=MESH)
        pl.semaphore_wait(barrier, len(near))

        @pl.loop(0, last + 1)
        def _(at):
            x_copy(at).start()
        for dst in (gw_ref, gs_ref, gb1_ref):
            dst[...] = jnp.zeros_like(dst)
        n = FF // 2
        moves = [(qo_ref.at[block(j, HALF)], wqkv.at[block(2 * j, HALF)]) for j in range(3)]
        moves += [(do_ref, wd.at[:HALF]), (to_ref, w2.at[:n]), (fo_ref, w1.at[:, :n])]
        tables = (n_scr, acc_scr, dh2_scr, dh1_scr, s_scr.at[0], s_scr.at[1])
        parts = [rp_ref.at[block(i, S)] for i in range(RING)] + [fp_ref.at[:, block(i, S)] for i in range(2)]
        copies = [pltpu.make_async_copy(src, dst, init_sem.at[i]) for i, (src, dst) in enumerate(moves + list(zip(parts, tables)))]
        for c in copies:
            c.start()
        for c in copies:
            c.wait()
        for j in range(3):
            wqkv[block(2 * j + 1, HALF), :] = tables[j // 2][block(j % 2, HALF), :].astype(BF16)
        wd[HALF:, :] = tables[1][HALF:, :].astype(BF16)
        for i in range(2):
            w2[block(2 + i, S), :] = tables[2 + i][...].astype(BF16)
            w1[:, block(2 + i, S)] = tables[RING + i][...].astype(BF16)

        x_copy(0).wait_recv()
        x_take(0).start()

    x_take(step).wait()

    @pl.when(step < last)
    def _():
        x_copy(step + 1).wait_recv()
        x_take(step + 1).start()

    def gx_copy(at, k):
        rows = pl.ds(pl.multiple_of(at * S, S), S)
        src, dst = gx_buf.at[at % 2, k], rows_ref.at[k, rows]
        if k:
            return pltpu.make_async_remote_copy(src, dst, gx_send.at[at % 2, k], gx_recv.at[at, k], device_id=z_device(k), device_id_type=MESH)
        return pltpu.make_async_copy(src, dst, gx_local.at[at % 2])

    def out_copy(at):
        return pltpu.make_async_remote_copy(out_buf.at[at % 2], peer_buf.at[at], out_send.at[at % 2], out_recv.at[at], device_id=peer, device_id_type=MESH)

    def own_store(at):
        return pltpu.make_async_copy(own_low.at[at % 2], out_ref.at[core * (last + 1) + at], own_sem.at[at % 2])

    def peer_store(at):
        return pltpu.make_async_copy(peer_low.at[at % 2], out_ref.at[(1 - core) * (last + 1) + at], peer_sem.at[at % 2])

    def drain(at):
        gx_copy(at, 0).wait()
        for k in range(1, RING):
            gx_copy(at, k).wait_send()
        out_copy(at).wait_send()
        own_store(at).wait()

    def take_peer(at):
        out_copy(at).wait_recv()

        @pl.when(at > 1)
        def _():
            peer_store(at - 2).wait()
        peer_low[at % 2] = peer_buf[at].astype(BF16)
        peer_store(at).start()

    @pl.when(step > 1)
    def _():
        drain(step - 2)

    cot = cot_ref[0]
    g1, b1, g2, b2, bd, bf = (vec_ref[i:i + 1, :].astype(F32) for i in range(6))
    bo = bd + bf

    def bias(row, i, n):
        width = HALF if row < 3 else FF // 2
        src, i = (bo_ref, i) if i < width // n else (bp_ref, i - width // n)
        return src[row:row + 1, block(i, n)]

    dctx_scr[...] = dot(cot, wd[...], NT).astype(BF16)
    cott_scr[...] = cot.T
    x = xo_ref[0].astype(F32) + xp_buf[slot]
    cen = x - jnp.mean(x, axis=-1, keepdims=True)
    inv = lax.rsqrt(jnp.mean(cen * cen, axis=-1, keepdims=True) + EPS)
    n = cen * inv
    n_scr[...] = n
    inv_scr[...] = inv
    h1_scr[...] = (n * g1 + b1).astype(BF16)
    h2_scr[...] = (n * g2 + b2).astype(BF16)
    gs_ref[4] += row_sums(cot.astype(F32))
    h1t_scr[...] = h1_scr[...].T
    h2t_scr[...] = h2_scr[...].T
    h1, h2 = h1_scr[...], h2_scr[...]

    for p in range(PAIRS):
        for j in range(3):
            v = dot(h1, wqkv[block(j * PAIRS + p, PAIR), :], NT) + bias(j, p, PAIR)
            v = v.astype(BF16)
            if j < 2:
                v = v.astype(F32)
                v = (v * rope_ref[0] + pltpu.roll(v, PAIR - ROT_HALF, 1) * rope_ref[1]
                     + pltpu.roll(v, ROT_HALF, 1) * rope_ref[2]).astype(BF16)
            qkv_scr[j, :, block(p, PAIR)] = v

    lane = lax.broadcasted_iota(jnp.int32, (HALF, PAIR), 1)
    causal = lax.broadcasted_iota(jnp.int32, (HALF, HALF), 0) >= lax.broadcasted_iota(jnp.int32, (HALF, HALF), 1)
    heads = (lane < HD, lane >= HD)
    zero = jnp.zeros((HALF, PAIR), BF16)

    def only(v, hh):
        return jnp.concatenate([jnp.where(heads[hh], v[block(i, HALF)], zero) for i in range(v.shape[0] // HALF)], axis=0)

    def rope_back(g, rows):
        g = rnd(g * HD ** -0.5)
        return (g * rope_ref[0, rows] + pltpu.roll(g * rope_ref[1, rows], ROT_HALF, 1)
                + pltpu.roll(g * rope_ref[2, rows], PAIR - ROT_HALF, 1)).astype(BF16)

    class Attention:
        def __init__(self, i):
            p, self.qb = i // 2, i % 2
            self.n, self.slot, self.lanes, self.rows = HALF * (self.qb + 1), self.qb, block(p, PAIR), block(self.qb, HALF)

        def operands(self):
            q, dc = qkv_scr[0, self.rows, self.lanes], dctx_scr[self.rows, self.lanes]
            return q, dc, qkv_scr[1, :self.n, self.lanes], qkv_scr[2, :self.n, self.lanes]

        def one(self):
            q, dc, k, v = self.operands()
            for hh in range(2):
                at = (self.slot, block(hh, HALF), slice(self.n))
                s_scr[at] = dot(only(q, hh), k, NT)
                dp_scr[at] = dot(only(dc, hh), v, NT).astype(BF16)

        def two(self):
            for hh in range(2):
                at = (self.slot, block(hh, HALF), slice(self.n))
                s = s_scr[at]
                diag = jnp.where(causal, s[:, self.n - HALF:], -1e30)
                s = jnp.concatenate([s[:, :HALF], diag], axis=1) if self.qb else diag
                e = jnp.exp2((s - jnp.max(s, axis=-1, keepdims=True)) * (HD ** -0.5 * LOG2E))
                pr = e * (1.0 / jnp.sum(e, axis=-1, keepdims=True))
                pb_scr[at] = pr.astype(BF16)
                dp = dp_scr[at].astype(F32)
                ds_scr[at] = (pr * (dp - jnp.sum(pr * dp, axis=-1, keepdims=True))).astype(BF16)

        def three(self):
            q, dc, k, v = self.operands()
            pb, ds = pb_scr[self.slot, :, :self.n], ds_scr[self.slot, :, :self.n]
            rows, lanes = self.rows, self.lanes
            ctx_scr[rows, lanes] = sum(dot(pb[block(hh, HALF)], only(v, hh)) for hh in range(2)).astype(BF16)
            dqkv_scr[0, rows, lanes] = rope_back(sum(dot(ds[block(hh, HALF)], only(k, hh)) for hh in range(2)), rows)
            dk = dot(ds, jnp.concatenate([only(q, hh) for hh in range(2)], axis=0), TN)
            dv = dot(pb, jnp.concatenate([only(dc, hh) for hh in range(2)], axis=0), TN)
            if not self.qb:
                dk_scr[...] = dk
                dv_scr[...] = dv
                return
            for b in range(2):
                at = block(b, HALF)
                gk, gv = (dk[at], dv[at]) if b else (dk[at] + dk_scr[...], dv[at] + dv_scr[...])
                dqkv_scr[1, at, lanes] = rope_back(gk, at)
                dqkv_scr[2, at, lanes] = gv.astype(BF16)

    class Mlp:
        def __init__(self, i):
            self.i, self.slot, self.cols = i, i % 2, block(i, HALF)

        def one(self):
            a_scr[self.slot] = dot(h2, w1[:, self.cols]) + bias(3, self.i, HALF)
            du_scr[self.slot] = dot(cot, w2[self.cols, :], NT).astype(BF16)

        def two(self):
            u, gp = gelu_parts(rnd(a_scr[self.slot]))
            da = (du_scr[self.slot].astype(F32) * gp).astype(BF16)
            u_scr[self.slot] = u.astype(BF16)
            da_scr[self.slot] = da
            gb1_ref[:, self.cols] += row_sums(da.astype(F32))

        def three(self):
            u, da = u_scr[self.slot], da_scr[self.slot]
            m, d = dot(u, w2[self.cols, :]), dot(da, w1[:, self.cols], NT)
            acc_scr[...] = acc_scr[...] + m if self.i else m
            dh2_scr[...] = dh2_scr[...] + d if self.i else d
            half, part = self.i // RING, 2 * S + self.i % RING * HALF
            gw_ref[:, wcol(half, part, HALF)] += dot(h2t_scr[...], da)
            gw_ref[:, wcol(half, part + 2 * S, HALF)] += dot(cott_scr[...], u)

    units = [u for i in range(2 * PAIRS) for u in (Attention(i), Mlp(i))]
    units[0].one()
    for i, u in enumerate(units):
        if i + 1 < len(units):
            units[i + 1].one()
        u.two()
        if i:
            units[i - 1].three()
    units[-1].three()

    dh1_scr[...] = sum(dot(dqkv_scr[j], wqkv[block(j, S), :]) for j in range(3))
    acc_scr[...] += dot(ctx_scr[...], wd[...])
    for half in range(2):
        hs = block(half, HALF)
        for j in range(3):
            gw_ref[:, wcol(half, j * HALF, HALF)] += dot(h1t_scr[...], dqkv_scr[j, :, hs])
        gw_ref[:, wcol(half, 3 * HALF, HALF)] += dot(cott_scr[...], ctx_scr[:, hs])

    n = n_scr[...]
    d1, d2 = rnd(dh1_scr[...]), rnd(dh2_scr[...])
    for i, v in zip((0, 1, 2, 3, 5, 6, 7), (d1 * n, d1, d2 * n, d2, *(dqkv_scr[j].astype(F32) for j in range(3)))):
        gs_ref[i] += row_sums(v)
    gn = d1 * g1 + d2 * g2
    s_scr[0] = cot.astype(F32) + inv_scr[...] * (
        gn - jnp.mean(gn, axis=-1, keepdims=True) - n * jnp.mean(gn * n, axis=-1, keepdims=True))
    low = (xo_ref[0].astype(F32) + xp_buf[slot] + (acc_scr[...] + bo)).astype(BF16)
    own_low[slot] = low
    out_buf[slot] = low.astype(F32)
    for k in range(RING):
        gx_buf[slot, k] = s_scr[0, :, pl.ds(pl.multiple_of((z + k) % RING * LANES, LANES), LANES)]
    for k in (2, 1, 3, 0):
        gx_copy(step, k).start()
    out_copy(step).start()
    own_store(step).start()

    @pl.when(step > 0)
    def _():
        take_peer(step - 1)

    @pl.when(step == last)
    def _():
        save = pltpu.make_async_copy(gw_ref, gw_out, init_sem.at[0])
        save.start()
        take_peer(step)
        for at in (step - 1, step):
            drain(at)
            peer_store(at).wait()

        @pl.loop(0, last + 1)
        def _(at):
            x_copy(at).wait_send()
            for k in range(1, RING):
                gx_copy(at, k).wait_recv()
        save.wait()


def rope_consts():
    lane = lax.broadcasted_iota(jnp.int32, (S, PAIR), 1) % HD
    inv_freq = ROPE_BASE ** (-(lane % ROT_HALF).astype(F32) / ROT_HALF)
    ang = lax.broadcasted_iota(F32, (S, PAIR), 0) * inv_freq
    sin, low, rot = jnp.sin(ang), lane < ROT_HALF, lane < 2 * ROT_HALF
    return jnp.stack([jnp.where(rot, jnp.cos(ang), 1.0), jnp.where(low, -sin, 0.0), jnp.where(rot & ~low, sin, 0.0)])


def layer_call(*args):
    count = args[0].shape[0]
    vm, hbm = pl.BlockSpec(memory_space=pltpu.VMEM), pl.BlockSpec(memory_space=pl.ANY)
    seq = pl.BlockSpec((1, S, D), lambda i: (i, 0, 0))
    own_seq = pl.BlockSpec((1, S, D), lambda i: (lax.axis_index('tp') * count + i, 0, 0))
    dma = pltpu.SemaphoreType.DMA

    def table(*lead):
        return pltpu.VMEM(lead + (S, D), F32)

    def low(*lead):
        return pltpu.VMEM(lead + (S, D), BF16)
    thin, thin_low, small = pltpu.VMEM((2, S, HALF), F32), pltpu.VMEM((2, S, HALF), BF16), pltpu.VMEM((HALF, PAIR), F32)
    return pl.pallas_call(
        layer_kernel,
        grid=(count,),
        in_specs=[seq, own_seq] + [vm] * 4 + [hbm] * (len(args) - 6),
        out_specs=[hbm] * 4 + [vm] * 2,
        out_shape=[jax.ShapeDtypeStruct((2 * count, S, D), BF16), jax.ShapeDtypeStruct((RING, count * S, LANES), F32), jax.ShapeDtypeStruct((count, S, D), F32),
                   jax.ShapeDtypeStruct((D, 2 * WIDE), F32), jax.ShapeDtypeStruct((ROW, ROW, D), F32), jax.ShapeDtypeStruct((ROW, FF), F32)],
        scratch_shapes=[pltpu.VMEM((D, 2 * WIDE), F32), pltpu.VMEM((3 * S, D), BF16), low(), pltpu.VMEM((D, FF), BF16), pltpu.VMEM((FF, D), BF16)] + [table()] * 4
        + [pltpu.VMEM((S, 1), F32)] + [low()] * 7 + [low(3)] * 2 + [table(2)] + [low(2)] * 3 + [thin] + [thin_low] * 3 + [small] * 2
        + [table(2), pltpu.VMEM((2, RING, S, LANES), F32), table(2), table(count)] + [low(2)] * 2
        + [dma((count,)), dma((count,)), dma((2,)), dma((2, RING)), dma((count, RING)), dma((2,)), dma((2,)), dma((count,)), dma((2,)), dma((2,)), dma((16,))],
        compiler_params=pltpu.CompilerParams(dimension_semantics=("arbitrary",), collective_id=1, has_side_effects=True,
                                             vmem_limit_bytes=VMEM_LIMIT),
        cost_estimate=pl.CostEstimate(flops=count * 30_000_000_000, bytes_accessed=60_000_000, transcendentals=0),
        name="layer",
    )(*args)


STEPS, UNROLL = 8, 8
STEP = PAD // STEPS


def table_kernel(half, ids_ref, rows_hbm, lo_ref, out_ref, lo_out_ref, rows_ref, acc, acc2, stage, lo_buf, sem, lo_in, lo_sent):
    load = pltpu.make_async_copy(rows_hbm, rows_ref, sem.at[0])
    load.start()

    @pl.loop(0, acc.shape[0] // LANES)
    def _(j):
        for a in (acc, acc2):
            a[pl.ds(pl.multiple_of(j * LANES, LANES), LANES), :] = jnp.zeros((LANES, LANES), F32)
    count, blocks = rows_ref.shape[1], lo_ref.shape[0]
    part = RING // 2 * count // blocks
    per = count // part

    def lo_load(i):
        return pltpu.make_async_copy(lo_ref.at[i], lo_buf.at[i % 2], lo_in.at[i % 2])

    def lo_store(i):
        return pltpu.make_async_copy(lo_buf.at[i % 2], lo_out_ref.at[i], lo_sent.at[i % 2])
    lo_load(0).start()
    load.wait()

    @pl.loop(0, blocks)
    def _(i):
        lo_load(i).wait()
        lo_store(i).start()

        @pl.when(i > 0)
        def _():
            lo_store(i - 1).wait()

        @pl.when(i + 1 < blocks)
        def _():
            lo_load(i + 1).start()
        k, first = i // per * 2, i % per * part

        @pl.loop(0, part // UNROLL)
        def _(g):
            t0 = pl.multiple_of(first + g * UNROLL, UNROLL)
            for j in range(UNROLL):
                for a, src in ((acc, k), (acc2, k + 1)):
                    row = pl.ds(ids_ref[src * count + t0 + j], 1)
                    a[row, :] += rows_ref[src, pl.ds(t0 + j, 1), :]
    lo_store(blocks - 1).wait()
    copies = []
    for i in range(2 * STEPS):
        h, c, slot = i // STEPS, i % STEPS, i % 2
        if i > 1:
            copies[i - 2].wait()

        @pl.loop(0, STEP // LANES, unroll=5)
        def _(b):
            at = pl.ds(pl.multiple_of(h * half + c * STEP + b * LANES, ROW), LANES)
            stage[slot, :, pl.ds(pl.multiple_of(b * LANES, LANES), LANES)] = (acc[at, :] + acc2[at, :]).T
        copies.append(pltpu.make_async_copy(stage.at[slot], out_ref.at[h, :, pl.ds(c * STEP, STEP)], sem.at[slot]))
        copies[i].start()
    for c in copies[-2:]:
        c.wait()


def table_call(ids, rows, lo, half):
    hbm, dma = pl.BlockSpec(memory_space=pl.ANY), pltpu.SemaphoreType.DMA((2,))
    return pl.pallas_call(
        functools.partial(table_kernel, half),
        grid_spec=pltpu.PrefetchScalarGridSpec(
            num_scalar_prefetch=1, grid=(), in_specs=[hbm] * 2, out_specs=[hbm] * 2,
            scratch_shapes=[pltpu.VMEM(rows.shape, F32)] + [pltpu.VMEM((half + PAD, LANES), F32)] * 2 + [pltpu.VMEM((2, LANES, STEP), F32), pltpu.VMEM((2, S, D), BF16)]
            + [dma] * 3),
        out_shape=[jax.ShapeDtypeStruct((2, LANES, PAD), F32), jax.ShapeDtypeStruct(lo.shape, lo.dtype)],
        compiler_params=pltpu.CompilerParams(vmem_limit_bytes=VMEM_LIMIT),
        cost_estimate=pl.CostEstimate(flops=4_000_000_000, bytes_accessed=34_000_000, transcendentals=0),
        name="table",
    )(ids, rows, lo)


def cut(lo, n):
    first = n // (2 * LANES) * LANES
    return (lo, first), (lo + first, n - first)


def over(lead, body, at=()):
    if not lead:
        return body(at)

    @pl.loop(0, lead[0])
    def _(i):
        over(lead[1:], body, at + (i,))


def add_into(dst, srcs, lead, lo, n):
    def body(at):
        v = dst[at + (slice(None), pl.ds(lo, n))]
        for s in srcs:
            v = v + s[at + (slice(None), pl.ds(0, n))]
        dst[at + (slice(None), pl.ds(lo, n))] = v
    over(lead, body)


def tail_kernel(t_ref, g_ref, e_ref, oute_ref, outw_ref, *scratch):
    tsum, tpeer, gsum, gpeer, send, recv, local = scratch[:7]
    bufs = list(scratch[7:])
    core, dp = lax.axis_index('tp'), lax.axis_index('dp')
    pos = {'z': dp // (RING * RING), 'y': dp // RING % RING, 'x': dp % RING}
    stride = {'z': RING * RING, 'y': RING, 'x': 1}

    def shift(axis, k):
        return (pos[axis] + k) % RING

    def device(axis, k):
        return (core, dp + (shift(axis, k) - pos[axis]) * stride[axis])
    peer = (1 - core, dp)

    barrier = pltpu.get_barrier_semaphore()
    near = [peer] + [device(axis, k) for axis in 'zyx' for k in (1, RING - 1)]
    for who in near:
        pl.semaphore_signal(barrier, inc=1, device_id=who, device_id_type=MESH)
    pl.semaphore_wait(barrier, len(near))

    used = [0, 0]

    def remote(src, dst, who):
        i = used[0]
        used[0] += 1
        c = pltpu.make_async_remote_copy(src, dst, send.at[i], recv.at[i], device_id=who, device_id_type=MESH)
        c.start()
        return c

    def load(src, dst):
        i = used[1]
        used[1] += 1
        c = pltpu.make_async_copy(src, dst, local.at[i])
        c.start()
        return c
    sent = []

    wide, extra, far = pl.ds(0, WIDE), pl.ds(WIDE, EXTRA), pl.ds(WIDE, WIDE)
    every = slice(None)
    py, px, pz = pos['y'], pos['x'], pos['z']
    width = COLOR // PARTS
    flows = {}
    for q in range(PARTS):
        for axis, lo in (('y', q * width), ('x', COLOR + q * width)):
            flows[lo] = axis
    pend = {}

    def piece(axis, i):
        return (i,) if axis in 'yz' else (every, i)

    def fetch(lo, k):
        axis = flows[lo]
        at = piece(axis, shift(axis, k)) + (every,) * (2 if axis == 'y' else 1) + (pl.ds(lo, width),)
        pend[lo, k] = [remote(t_ref.at[(1,) + at], tpeer.at[at], peer), load(t_ref.at[(0,) + at], tsum.at[at])]

    def fetch_g(k):
        i = shift('z', k)
        pend['g', k] = [remote(g_ref.at[i, every, every, every, far], gpeer.at[i, every, every, every, wide], peer),
                        load(g_ref.at[i, every, every, every, wide], gsum.at[i, every, every, every, wide])]
    order = list(flows)
    for k in (2, 1, RING - 1, 0):
        for n, lo in enumerate(order):
            fetch(lo, k)
            if n == 1:
                if k == 2:
                    pend['e'] = [remote(e_ref.at[1], gpeer.at[every, every, every, every, extra], peer),
                                 load(e_ref.at[0], gsum.at[every, every, every, every, extra])]
                fetch_g(k)

    def arrive(key):
        out, here = pend[key]
        sent.append(out)
        out.wait_recv()
        here.wait()

    def ready(name, k):
        arrive((name, k))
        if name == 'g':
            i = shift('z', k)
            add_into(gsum.at[i], [gpeer.at[i]], (RING, RING), 0, GCOLS)
            return
        axis = flows[name]
        at = piece(axis, shift(axis, k))
        v = at + (every,) * (2 if axis == 'y' else 1) + (pl.ds(name, width),)
        add_into(tsum.at[at], [tpeer.at[v]], (RING,), name, width)

    class Stage:
        def __init__(self, axis, piece, lead, lo, n, need=None):
            self.axis, self.piece, self.lead, self.lo, self.n, self.need = axis, piece, lead, lo, n, need
            self.halves = cut(lo, n)
            self.near = [bufs.pop(0), bufs.pop(0)]
            self.last = [bufs.pop(0), bufs.pop(0)]

        def view(self, k, lo, n):
            return self.piece(shift(self.axis, k)).at[(every,) * (len(self.lead) + 1) + (pl.ds(lo, n),)]

        def want(self, k):
            if self.need is not None:
                ready(self.need, k)

        def first(self):
            self.want(2)
            self.c1 = [remote(self.view(2, *self.halves[s]), self.near[s], device(self.axis, k))
                       for s, k in enumerate((1, RING - 1))]

        def second(self):
            self.want(1)
            self.want(RING - 1)
            self.c2 = []
            for s, k in enumerate((1, RING - 1)):
                self.c1[s].wait_recv()
                add_into(self.piece(shift(self.axis, k)), [self.near[s]], self.lead, *self.halves[s])
                self.c2.append(remote(self.view(k, self.lo, self.n), self.last[s], device(self.axis, k)))

        def finish(self):
            self.want(0)
            for c in self.c2:
                c.wait_recv()
            add_into(self.piece(shift(self.axis, 0)), self.last, self.lead, self.lo, self.n)
            sent.extend(self.c1 + self.c2)

    one, two = (RING,), (RING, RING)
    rows_y, rows_x = (lambda i: tsum.at[i]), (lambda i: tsum.at[:, i])
    last_x, last_y = (lambda i: tsum.at[py, i]), (lambda i: tsum.at[i, px])
    first = [Stage(axis, rows_y if axis == 'y' else rows_x, one, lo, width, lo) for lo, axis in flows.items()]
    g1 = Stage('z', lambda i: gsum.at[i], two, 0, GCOLS, 'g')
    second = [Stage('x' if axis == 'y' else 'y', last_x if axis == 'y' else last_y, (), lo, width) for lo, axis in flows.items()]
    (c0, cn), (d0, dn) = cut(0, GCOLS)
    c1 = Stage('y', lambda i: gsum.at[pz, i], one, c0, cn)
    d1 = Stage('x', lambda i: gsum.at[pz, :, i], one, d0, dn)
    c2 = Stage('x', lambda i: gsum.at[pz, py, i], (), c0, cn)
    d2 = Stage('y', lambda i: gsum.at[pz, i, px], (), d0, dn)

    firsts = first[:2] + [g1] + first[2:]
    after = dict(zip(first, ([s] for s in second)))
    after[g1] = [c1, d1]
    for s in firsts:
        if s is g1:
            arrive('e')
        s.first()
    for s in firsts:
        s.second()
    for s in firsts:
        s.finish()
        for t in after[s]:
            t.first()
    nexts = [t for s in firsts for t in after[s]]
    for s in nexts:
        s.second()
    for s, t in ((c1, c2), (d1, d2)):
        s.finish()
        t.first()
    for s in second:
        s.finish()
    oute_ref[...] = tsum[py, px, :, 0:oute_ref.shape[1]]
    for s in (c2, d2):
        s.second()
    for s in (c2, d2):
        s.finish()
    outw_ref[...] = gsum[pz, py, px]
    for c in sent:
        c.wait_send()


def tail_call(t, g, e, rows):
    def ring_bufs(lead, n):
        (_, p), (_, q) = cut(0, n)
        return [pltpu.VMEM(lead + (ROW, w), F32) for w in (p, q, n, n)]
    (_, cn), (_, dn) = cut(0, GCOLS)
    one, two, three = (RING,), (RING,) * 2, (RING,) * 3
    width = COLOR // PARTS
    bufs = sum((ring_bufs(*b) for b in [(one, width)] * (2 * PARTS) + [(two, GCOLS)] + [((), width)] * (2 * PARTS)
                + [(one, cn), (one, dn), ((), cn), ((), dn)]), [])
    dma = pltpu.SemaphoreType.DMA
    hbm = pl.BlockSpec(memory_space=pl.ANY)
    vm = pl.BlockSpec(memory_space=pltpu.VMEM)
    return pl.pallas_call(
        tail_kernel,
        in_specs=[hbm] * 3, out_specs=[vm] * 2,
        out_shape=[jax.ShapeDtypeStruct((ROW, rows), F32), jax.ShapeDtypeStruct((ROW, GCOLS), F32)],
        scratch_shapes=[pltpu.VMEM(two + (ROW, PAD), F32)] * 2 + [pltpu.VMEM(three + (ROW, GCOLS), F32)] * 2
        + [dma((128,)), dma((128,)), dma((32,))] + bufs,
        compiler_params=pltpu.CompilerParams(collective_id=0, has_side_effects=True, vmem_limit_bytes=VMEM_LIMIT),
        name="tail",
    )(t, g, e)


def solution(mesh):
    tp, dp, no = 'tp', 'dp', None
    one, vec_dp, both = P(no), P(dp), P((tp, dp))
    arg_specs = (P(dp, no), P(tp, no), one, one, one, one, P(no, tp, no, no), P(tp, no, no), P(tp, no, no), one, P(no, tp), P(tp), P(tp, no), one, P(dp, no, no))
    out_specs = (P(dp, no, no), P(tp, dp), vec_dp, vec_dp, vec_dp, vec_dp, P(dp, tp, no, no), both, P(tp, no, dp), vec_dp, P(dp, tp), both, P(tp, dp), vec_dp)
    chips = mesh.shape[dp]
    plane = chips // RING

    def swap(v):
        return lax.ppermute(v, tp, [(0, 1), (1, 0)])

    def z_shift(v, k):
        return lax.ppermute(v, dp, [(i, (i + k * plane) % chips) for i in range(chips)]) if k else v

    def device_step(token_ids, embed_table, ln1_gain, ln1_bias, ln2_gain, ln2_bias, w_qkv, b_qkv, w_dense, b_dense, w_fc1, b_fc1, w_fc2, b_fc2, cotangent):
        core = lax.axis_index(tp)
        vocab_local = embed_table.shape[0]
        seqs = token_ids.shape[0] // 2
        f = lambda v: v.astype(F32)

        wq_own = w_qkv.transpose(2, 1, 3, 0).reshape(3 * HALF, D)
        wd_own = w_dense.reshape(HALF, D)
        rows_peer = swap(f(jnp.concatenate([wq_own, wd_own, w_fc2], axis=0)))
        fc1_peer = swap(f(w_fc1))
        wide = FF // 2
        bias = f(jnp.concatenate([jnp.pad(b_qkv.transpose(1, 0, 2).reshape(3, HALF), ((0, 0), (0, wide - HALF))), b_fc1.reshape(1, wide)], axis=0))
        bias_peer = swap(bias)
        vec = jnp.stack([ln1_gain, ln1_bias, ln2_gain, ln2_bias, b_dense, b_fc2])

        tokens = jnp.where(core == 0, token_ids, jnp.roll(token_ids, seqs, axis=0)).reshape(-1)
        local = tokens - core * vocab_local
        codes = jnp.where((local >= 0) & (local < vocab_local), local, vocab_local)
        x_send, x_own = look_up_call(codes, embed_table)
        flat = tokens[:seqs * S]
        ids = jnp.concatenate([z_shift(flat, k) for k in range(RING)]) - core * vocab_local

        args = (x_own, cotangent, vec, bias, bias_peer, rope_consts(), x_send, wq_own, wd_own, w_fc1, w_fc2, rows_peer, fc1_peer)
        layer_out, rows, _, grad_w, grad_s, grad_b1 = layer_call(*args)

        dense, layer_out = table_call(jnp.where(ids < 0, ids + 2 * vocab_local, ids), rows, layer_out, vocab_local)

        small = jnp.sum(grad_s, axis=1)
        norms = small[:5].reshape(5, chips, ROW).transpose(1, 0, 2).reshape(chips, 5 * ROW)
        grad_bq = small[5:].reshape(3, 2, PAIRS, HD).transpose(1, 2, 0, 3).reshape(2, chips, -1)
        grad_bf = jnp.sum(grad_b1, axis=0).reshape(2, chips, -1)
        extra = jnp.concatenate([jnp.stack([norms, norms]), grad_bq, grad_bf], axis=2)
        ends = (5 * ROW, 5 * ROW + grad_bq.shape[2], extra.shape[2])
        extra = jnp.pad(extra[:, :, None, :], ((0, 0), (0, 0), (0, ROW - 1), (0, EXTRA - ends[2])))
        ring3 = (RING,) * 3
        sum_embed, total = tail_call(dense.reshape(2, RING, RING, ROW, PAD), grad_w.reshape(ring3 + (ROW, 2 * WIDE)),
                                     extra.reshape((2,) + ring3 + (ROW, EXTRA)), vocab_local)
        qkv = 3 * HALF
        sum_wqkv = total[:, :qkv].reshape(ROW, 3, PAIRS, HD).transpose(0, 2, 1, 3)
        sum_wdense = total[:, qkv:wide].reshape(ROW, PAIRS, HD).transpose(1, 2, 0)
        sum_wfc1, sum_wfc2 = total[:, wide:2 * wide], total[:, 2 * wide:WIDE].T
        last = total[0, WIDE:]
        n1g, n1b, n2g, n2b, bias = last[:ends[0]].reshape(5, ROW)
        return (layer_out, sum_embed.T, n1g, n1b, n2g, n2b, sum_wqkv, last[ends[0]:ends[1]], sum_wdense, bias, sum_wfc1,
                last[ends[1]:ends[2]], sum_wfc2, bias)

    return jax.shard_map(device_step, mesh=mesh, in_specs=arg_specs, out_specs=out_specs, check_vma=False)
```

profile of v0, /device:TPU:0, one launch (start us, length us, event | category | flops | bytes accessed | tf_op | source)
XLA Modules:
  0.0 404.2 jit_solution(8681361499983176161)
XLA Ops:
  0.6 0.0 copy-start.1
  0.7 0.8 fusion.15
  1.5 0.8 subtract_bitcast_fusion
  2.3 2.1 collective-permute-start
  4.4 3.6 collective-permute-start.1
  8.0 1.0 collective-permute-start.2
  9.0 1.2 copy.31
  10.2 0.0 copy-start
  10.2 4.1 %maximum_convert_fusion = f32[2048,512]{1,0:T(8,128)} fusion(bf16[1024,512]{1,0:T(8,128)(2,1)} %to_ref.1, bf16[256,512]{1,0:T(8,128)(2,1)} %bitcast.48, bf16[768,512]{1,0:T(8,128)(2,1)S(1)} %bitcast.42), kind=kLoop, calls=%fused_computation | loop fusion | flops 6291456 | bytes 6291456 | tf_op jit(solution)/shard_map/convert_element_type | solution.py:712
  14.3 0.0 collective-permute-start.4
  14.3 0.0 copy-done.1
  14.3 1.6 convert_element_type.38
  15.9 0.0 copy-done
  15.9 0.5 collective-permute-start.5
  16.5 0.6 and_select_fusion.codes_ref
  17.1 34.5 %look_up.1 = (f32[8,512,512]{2,1,0:T(8,128)}, bf16[8,512,512]{2,1,0:T(8,128)(2,1)}) custom-call(s32[8192]{0:T(1024)} %and_select_fusion.codes_ref, bf16[25152,512]{1,0:T(8,128)(2,1)} %table_ref.1), custom_call_target="tpu_custom_call" | custom-call | flops 40000000000 | bytes 40000000 | tf_op jit(solution)/shard_map/look_up/pallas_call | solution.py:86
  51.6 0.0 copy-done.4
  51.6 0.0 copy-done.3
  51.6 0.1 reshape.368
  51.7 1.0 fusion.1
  52.7 0.9 pad_maximum_fusion.rope_ref
  53.7 0.0 copy-done.5
  53.7 0.0 copy-start.2
  53.7 0.0 copy-done.6
  53.7 0.7 stack.32
  54.4 0.7 stack.33
  55.1 0.7 stack.34
  55.8 0.7 stack.35
  56.5 0.6 stack.36.vec_ref
  57.1 0.0 collective-permute-done
  57.1 0.0 collective-permute-start.3
  57.1 0.0 collective-permute-done.1
  57.1 0.0 collective-permute-done.2
  57.1 1.4 compare_select_fusion.ids_ref
  58.5 0.0 collective-permute-done.3.bp_ref
  58.5 0.6 copy-done.8
  59.1 0.0 collective-permute-done.5.fp_ref
  59.1 0.0 collective-permute-done.4.rp_ref
  59.1 0.0 copy-done.2
  59.1 178.5 %layer.1 = (bf16[16,512,512]{2,1,0:T(8,128)(2,1)}, f32[4,4096,128]{2,1,0:T(8,128)}, f32[8,512,512]{2,1,0:T(8,128)}, f32[512,6144]{1,0:T(8,128)}, f32[8,8,512]{2,1,0:T(8,128)}, /*index=5*/f32[8,2048]{1,0:T(8,128)}) custom-call(bf16[8,512,512]{2,1,0:T(8,128)(2,1)} %get-tuple-element.25.xo_ref, bf16[16,512,512]{2,1,0:T(8,128)(2,1)} %cot_ref.1, ...), custom_call_target="tpu_custom_call" | custom-call | flops 240000008192 | bytes 60000000 | tf_op jit(solution)/shard_map/layer/pallas_call | solution.py:389
  237.6 0.9 reduce_sum.18
  238.6 0.1 reshape.374
  238.7 0.1 copy.32
  238.8 0.1 reshape.375
  238.9 0.1 reshape.376
  239.0 0.1 copy.34
  239.1 0.9 reduce_sum.19
  240.0 0.1 reshape.377
  240.1 0.1 copy.35
  240.2 0.1 copy.38
  240.2 0.8 pad.9.clone
  241.1 57.4 %table.1 = (f32[2,128,25600]{2,1,0:T(8,128)}, bf16[16,512,512]{2,1,0:T(8,128)(2,1)}) custom-call(s32[16384]{0:T(1024)} %compare_select_fusion.ids_ref, f32[4,4096,128]{2,1,0:T(8,128)} %get-tuple-element.27.rows_hbm, bf16[16,512,512]{2,1,0:T(8,128)(2,1)} %get-tuple-element.28.lo_ref), custom_call_target="tpu_custom_call" | custom-call | flops 4000000000 | bytes 34000000 | tf_op jit(solution)/shard_map/table/pallas_call | solution.py:471
  298.5 94.9 %tail.1 = (f32[8,25152]{1,0:T(8,128)}, f32[8,3200]{1,0:T(8,128)}) custom-call(f32[2,4,4,8,25600]{4,3,2,1,0:T(8,128)} %bitcast.40, f32[4,4,4,8,6144]{4,3,2,1,0:T(8,128)} %bitcast.41, f32[2,4,4,4,8,128]{5,4,3,2,1,0:T(8,128)} %bitcast.44), custom_call_target="tpu_custom_call" | custom-call | tf_op jit(solution)/shard_map/tail/pallas_call | solution.py:683
  393.4 0.7 slice.66
  394.2 1.4 slice_bitcast_fusion
  395.6 0.7 slice.69
  396.3 1.5 slice_bitcast_fusion.3
  397.7 1.3 slice_bitcast_fusion.2
  399.0 1.3 slice_bitcast_fusion.4
  400.2 0.7 reshape.379
  400.9 0.1 reshape.380
  401.0 0.6 copy.42
  401.6 0.5 copy.45
  402.1 2.1 copy.46
  (19 shorter events, 0.1 us)
Async XLA Ops:
  0.6 13.7 %copy-start.1 = (bf16[512,1024]{1,0:T(8,128)(2,1)S(1)}, bf16[512,1024]{1,0:T(8,128)(2,1)}, u32[]{:S(2)}) copy-start(bf16[512,1024]{1,0:T(8,128)(2,1)} %fo_ref.1) | copy-start | bytes 3145732
  2.3 54.8 %collective-permute-start = (s32[4096]{0:T(1024)S(1)}, s32[4096]{0:T(1024)}, u32[]{:S(2)}, u32[]{:S(2)}) collective-permute-start(s32[4096]{0:T(1024)S(1)} %bitcast.53), channel_id=1, source_target_pairs={{0,16},{1,17},{2,18},{3,19},{4,20},{5,21},{6,22},{7,23},{8,24},{9,... | collective-permute-start | bytes 49160 | tf_op jit(solution)/shard_map/ppermute | solution.py:706
  4.4 52.7 %collective-permute-start.1 = (s32[4096]{0:T(1024)S(1)}, s32[4096]{0:T(1024)}, u32[]{:S(2)}, u32[]{:S(2)}) collective-permute-start(s32[4096]{0:T(1024)S(1)} %bitcast.54), channel_id=1, source_target_pairs={{0,32},{1,33},{2,34},{3,35},{4,36},{5,37},{6,38},{7,39},{8,40},{9,... | collective-permute-start | bytes 49160 | tf_op jit(solution)/shard_map/ppermute | solution.py:706
  8.0 49.1 %collective-permute-start.2 = (s32[4096]{0:T(1024)S(1)}, s32[4096]{0:T(1024)}, u32[]{:S(2)}, u32[]{:S(2)}) collective-permute-start(s32[4096]{0:T(1024)S(1)} %bitcast.55), channel_id=1, source_target_pairs={{0,48},{1,49},{2,50},{3,51},{4,52},{5,53},{6,54},{7,55},{8,56},{9,... | collective-permute-start | bytes 49160 | tf_op jit(solution)/shard_map/ppermute | solution.py:706
  10.2 5.7 %copy-start = (bf16[3,4,64,512]{3,2,1,0:T(8,128)(2,1)}, bf16[3,4,64,512]{3,2,1,0:T(8,128)(2,1)S(1)}, u32[]{:S(2)}) copy-start(bf16[3,4,64,512]{3,2,1,0:T(8,128)(2,1)S(1)} %copy.31) | copy-start | bytes 2359300
  14.3 44.8 %collective-permute-start.4 = (f32[2048,512]{1,0:T(8,128)}, f32[2048,512]{1,0:T(8,128)}, u32[]{:S(2)}, u32[]{:S(2)}) collective-permute-start(f32[2048,512]{1,0:T(8,128)} %maximum_convert_fusion), channel_id=1, source_target_pairs={{0,64},{64,0},{1,65},{65,1},{2,66},{66,2},{3,67},{67,3},{4,68},{68... | collective-permute-start | bytes 12582920 | tf_op jit(solution)/shard_map/ppermute | solution.py:703
  15.9 43.2 %collective-permute-start.5 = (f32[512,1024]{1,0:T(8,128)}, f32[512,1024]{1,0:T(8,128)}, u32[]{:S(2)}, u32[]{:S(2)}) collective-permute-start(f32[512,1024]{1,0:T(8,128)} %convert_element_type.38), channel_id=1, source_target_pairs={{0,64},{64,0},{1,65},{65,1},{2,66},{66,2},{3,67},{67,3},{4,68},{68... | collective-permute-start | bytes 6291464 | tf_op jit(solution)/shard_map/ppermute | solution.py:703
  17.1 34.5 %copy-start.4 = (bf16[1024]{0:T(1024)(128)(2,1)S(1)}, bf16[1024]{0:T(1024)(128)(2,1)}, u32[]{:S(2)}) copy-start(bf16[1024]{0:T(1024)(128)(2,1)} %param.26) | copy-start | bytes 6148
  17.1 34.5 %copy-start.3 = (bf16[4,3,64]{2,0,1:T(4,128)(2,1)S(1)}, bf16[4,3,64]{2,0,1:T(4,128)(2,1)}, u32[]{:S(2)}) copy-start(bf16[4,3,64]{2,0,1:T(4,128)(2,1)} %param.22) | copy-start | bytes 4612
  17.1 36.6 %copy-start.5 = (bf16[512]{0:T(512)(128)(2,1)S(1)}, bf16[512]{0:T(512)(128)(2,1)}, u32[]{:S(2)}) copy-start(bf16[512]{0:T(512)(128)(2,1)} %param.17) | copy-start | bytes 3076
  17.1 36.6 %copy-start.6 = (bf16[512]{0:T(512)(128)(2,1)S(1)}, bf16[512]{0:T(512)(128)(2,1)}, u32[]{:S(2)}) copy-start(bf16[512]{0:T(512)(128)(2,1)} %param.18) | copy-start | bytes 3076
  53.7 5.4 %copy-start.2 = (f32[4,1024]{1,0:T(4,128)}, f32[4,1024]{1,0:T(4,128)S(1)}, u32[]{:S(2)}) copy-start(f32[4,1024]{1,0:T(4,128)S(1)} %fusion.14.bo_ref) | copy-start | bytes 49156
  57.1 1.4 collective-permute-start.3
  58.5 0.6 copy-start.8
  397.7 6.5 %copy-start.7 = (f32[8]{0:T(128)}, f32[8]{0:T(128)S(1)}, u32[]{:S(2)}) copy-start(f32[8]{0:T(128)S(1)} %get-tuple-element.103) | copy-start | bytes 100
where the time goes:
time: 405 us; the launch traced here: 404 us
  Pallas kernels  365 us (90%)
  local copies, waits for them, and re-layouts  18.5 us (5%)
  other arithmetic  12.3 us (3%)
  starting transfers between devices  7.24 us (2%)
    pallas_call x1, Pallas kernels, layer_call(): pl.pallas_call(layer_kernel, grid=(count,), in_specs=[seq, own_seq] + [vm...  178 us
    pallas_call x1, Pallas kernels, tail_call(): pl.pallas_call(tail_kernel, in_specs=[hbm] * 3, out_specs=[vm] * 2, out_s...  94.9 us
    pallas_call x1, Pallas kernels, table_call(): pl.pallas_call(functools.partial(table_kernel, half), grid_spec=pltpu.Pre...  57.4 us
    pallas_call x1, Pallas kernels, look_up_call(): pl.pallas_call(look_up_kernel, grid_spec=pltpu.PrefetchScalarGridSpec(num...  34.5 us
  transfers between devices with their start and end apart: 6, of which 0 were waited for; matrix products, arithmetic and copies ran while one was open for 4% of the time, Pallas kernels for 9%

commit v1 on v0

--- a/solution.py
+++ b/solution.py
@@ -13,6 +13,7 @@
 TN = (((0,), (0,)), ((), ()))
 S, D, FF, HEADS, HD = 512, 512, 2048, 8, 64
 PAIR, HALF, PAIRS, FF_STEPS, ROT_HALF = 2 * HD, S // 2, HEADS // 2, FF // S, HD // 8
+QKV, BOTH = 3, range(2)
 EPS, ROPE_BASE = 1e-5, 10000.0
 LOG2E = 1.4426950408889634
 SQRT_HALF, INV_SQRT_2PI = 0.7071067811865476, 0.3989422804014327
@@ -58,10 +59,10 @@
 
     @pl.when(step == 0)
     def _():
-        rows = table_ref.shape[0]
-        load = pltpu.make_async_copy(table_ref, table.at[:rows], sem)
+        tiles = table_ref.shape[0]
+        load = pltpu.make_async_copy(table_ref, table.at[:tiles], sem)
         load.start()
-        table[rows:, :] = jnp.zeros((ROW, D), BF16)
+        table[tiles] = jnp.zeros((ROW, D), BF16)
         load.wait()
     sub = lax.broadcasted_iota(jnp.int32, (ROW, D), 0)
 
@@ -69,8 +70,7 @@
         got = jnp.zeros((ROW, D), F32)
         for j in range(ROW):
             at = codes_ref[first + j]
-            rows = table[pl.ds(pl.multiple_of(at & -ROW, ROW), ROW), :].astype(F32)
-            got = jnp.where(sub == j, pltpu.roll(rows, (j - at) & (ROW - 1), 0), got)
+            got = jnp.where(sub == j, pltpu.roll(table[at >> 3].astype(F32), at & (ROW - 1), 0), got)
         return got
 
     for k, dst in enumerate((own_ref, peer_ref)):
@@ -87,7 +87,7 @@
         look_up_kernel,
         grid_spec=pltpu.PrefetchScalarGridSpec(
             num_scalar_prefetch=1, grid=(seqs,), in_specs=[pl.BlockSpec(memory_space=pl.ANY)], out_specs=[seq] * 2,
-            scratch_shapes=[pltpu.VMEM((table.shape[0] + ROW, D), BF16), pltpu.SemaphoreType.DMA]),
+            scratch_shapes=[pltpu.VMEM((table.shape[0] + 1, ROW, D), BF16), pltpu.SemaphoreType.DMA]),
         out_shape=[jax.ShapeDtypeStruct((seqs, S, D), t) for t in (F32, BF16)],
         compiler_params=pltpu.CompilerParams(dimension_semantics=("arbitrary",), vmem_limit_bytes=VMEM_LIMIT),
         cost_estimate=pl.CostEstimate(flops=40_000_000_000, bytes_accessed=40_000_000, transcendentals=0),
@@ -95,11 +95,11 @@
     )(codes, table)
 
 
-def layer_kernel(xo_ref, cot_ref, vec_ref, bo_ref, bp_ref, rope_ref, xs_ref, qo_ref, do_ref, fo_ref, to_ref, rp_ref, fp_ref,
-                 out_ref, rows_ref, xin_ref, gw_out, gs_ref, gb1_ref,
-                 gw_ref, wqkv, wd, w1, w2, n_scr, acc_scr, dh2_scr, dh1_scr, inv_scr, h1_scr, h2_scr, h1t_scr, h2t_scr, cott_scr, dctx_scr, ctx_scr,
+def layer_kernel(xo_ref, cot_ref, g1_ref, b1_ref, g2_ref, b2_ref, bd_ref, bf_ref, bo_ref, bp_ref, rope_ref, xs_ref, ids_ref, qo_ref, do_ref, fo_ref, to_ref, rp_ref, fp_ref,
+                 out_ref, rows_ref, xin_ref, idz_ref, gw_out, gs_out, gb1_out,
+                 gw_ref, gs_ref, gb1_ref, wqkv, wd, w1, w2, n_scr, acc_scr, dh2_scr, dh1_scr, inv_scr, h1_scr, h2_scr, h1t_scr, h2t_scr, cott_scr, dctx_scr, ctx_scr,
                  qkv_scr, dqkv_scr, s_scr, dp_scr, pb_scr, ds_scr, a_scr, du_scr, u_scr, da_scr, dk_scr, dv_scr,
-                 xp_buf, gx_buf, out_buf, peer_buf, own_low, peer_low, x_send, x_recv, x_load, gx_send, gx_recv, gx_local, out_send, out_recv, own_sem, peer_sem, init_sem):
+                 xp_buf, gx_buf, out_buf, peer_buf, own_low, peer_low, x_send, x_recv, x_load, id_send, id_recv, gx_send, gx_recv, gx_local, out_send, out_recv, own_sem, peer_sem, init_sem):
     step, last = pl.program_id(0), pl.num_programs(0) - 1
     slot = step % 2
     core, chip = lax.axis_index('tp'), lax.axis_index('dp')
@@ -115,6 +115,11 @@
 
     def x_take(at):
         return pltpu.make_async_copy(xin_ref.at[at], xp_buf.at[at % 2], x_load.at[at % 2])
+
+    def id_copy(k):
+        if k:
+            return pltpu.make_async_remote_copy(ids_ref, idz_ref.at[k], id_send.at[k], id_recv.at[k], device_id=z_device(k), device_id_type=MESH)
+        return pltpu.make_async_copy(ids_ref, idz_ref.at[k], id_send.at[k])
 
     @pl.when(step == 0)
     def _():
@@ -127,22 +132,24 @@
         @pl.loop(0, last + 1)
         def _(at):
             x_copy(at).start()
+        for k in range(RING):
+            id_copy(k).start()
         for dst in (gw_ref, gs_ref, gb1_ref):
             dst[...] = jnp.zeros_like(dst)
         n = FF // 2
-        moves = [(qo_ref.at[block(j, HALF)], wqkv.at[block(2 * j, HALF)]) for j in range(3)]
+        moves = [(qo_ref.at[block(j, HALF)], wqkv.at[block(2 * j, HALF)]) for j in range(QKV)]
         moves += [(do_ref, wd.at[:HALF]), (to_ref, w2.at[:n]), (fo_ref, w1.at[:, :n])]
         tables = (n_scr, acc_scr, dh2_scr, dh1_scr, s_scr.at[0], s_scr.at[1])
-        parts = [rp_ref.at[block(i, S)] for i in range(RING)] + [fp_ref.at[:, block(i, S)] for i in range(2)]
+        parts = [rp_ref.at[block(i, S)] for i in range(RING)] + [fp_ref.at[:, block(i, S)] for i in BOTH]
         copies = [pltpu.make_async_copy(src, dst, init_sem.at[i]) for i, (src, dst) in enumerate(moves + list(zip(parts, tables)))]
         for c in copies:
             c.start()
         for c in copies:
             c.wait()
-        for j in range(3):
+        for j in range(QKV):
             wqkv[block(2 * j + 1, HALF), :] = tables[j // 2][block(j % 2, HALF), :].astype(BF16)
         wd[HALF:, :] = tables[1][HALF:, :].astype(BF16)
-        for i in range(2):
+        for i in BOTH:
             w2[block(2 + i, S), :] = tables[2 + i][...].astype(BF16)
             w1[:, block(2 + i, S)] = tables[RING + i][...].astype(BF16)
 
@@ -193,7 +200,7 @@
         drain(step - 2)
 
     cot = cot_ref[0]
-    g1, b1, g2, b2, bd, bf = (vec_ref[i:i + 1, :].astype(F32) for i in range(6))
+    g1, b1, g2, b2, bd, bf = (v[...].astype(F32).reshape(1, D) for v in (g1_ref, b1_ref, g2_ref, b2_ref, bd_ref, bf_ref))
     bo = bd + bf
 
     def bias(row, i, n):
@@ -217,7 +224,7 @@
     h1, h2 = h1_scr[...], h2_scr[...]
 
     for p in range(PAIRS):
-        for j in range(3):
+        for j in range(QKV):
             v = dot(h1, wqkv[block(j * PAIRS + p, PAIR), :], NT) + bias(j, p, PAIR)
             v = v.astype(BF16)
             if j < 2:
@@ -250,13 +257,13 @@
 
         def one(self):
             q, dc, k, v = self.operands()
-            for hh in range(2):
+            for hh in BOTH:
                 at = (self.slot, block(hh, HALF), slice(self.n))
                 s_scr[at] = dot(only(q, hh), k, NT)
                 dp_scr[at] = dot(only(dc, hh), v, NT).astype(BF16)
 
         def two(self):
-            for hh in range(2):
+            for hh in BOTH:
                 at = (self.slot, block(hh, HALF), slice(self.n))
                 s = s_scr[at]
                 diag = jnp.where(causal, s[:, self.n - HALF:], -1e30)
@@ -271,15 +278,15 @@
             q, dc, k, v = self.operands()
             pb, ds = pb_scr[self.slot, :, :self.n], ds_scr[self.slot, :, :self.n]
             rows, lanes = self.rows, self.lanes
-            ctx_scr[rows, lanes] = sum(dot(pb[block(hh, HALF)], only(v, hh)) for hh in range(2)).astype(BF16)
-            dqkv_scr[0, rows, lanes] = rope_back(sum(dot(ds[block(hh, HALF)], only(k, hh)) for hh in range(2)), rows)
-            dk = dot(ds, jnp.concatenate([only(q, hh) for hh in range(2)], axis=0), TN)
-            dv = dot(pb, jnp.concatenate([only(dc, hh) for hh in range(2)], axis=0), TN)
+            ctx_scr[rows, lanes] = sum(dot(pb[block(hh, HALF)], only(v, hh)) for hh in BOTH).astype(BF16)
+            dqkv_scr[0, rows, lanes] = rope_back(sum(dot(ds[block(hh, HALF)], only(k, hh)) for hh in BOTH), rows)
+            dk = dot(ds, jnp.concatenate([only(q, hh) for hh in BOTH], axis=0), TN)
+            dv = dot(pb, jnp.concatenate([only(dc, hh) for hh in BOTH], axis=0), TN)
             if not self.qb:
                 dk_scr[...] = dk
                 dv_scr[...] = dv
                 return
-            for b in range(2):
+            for b in BOTH:
                 at = block(b, HALF)
                 gk, gv = (dk[at], dv[at]) if b else (dk[at] + dk_scr[...], dv[at] + dv_scr[...])
                 dqkv_scr[1, at, lanes] = rope_back(gk, at)
@@ -319,17 +326,17 @@
             units[i - 1].three()
     units[-1].three()
 
-    dh1_scr[...] = sum(dot(dqkv_scr[j], wqkv[block(j, S), :]) for j in range(3))
+    dh1_scr[...] = sum(dot(dqkv_scr[j], wqkv[block(j, S), :]) for j in range(QKV))
     acc_scr[...] += dot(ctx_scr[...], wd[...])
-    for half in range(2):
+    for half in BOTH:
         hs = block(half, HALF)
-        for j in range(3):
+        for j in range(QKV):
             gw_ref[:, wcol(half, j * HALF, HALF)] += dot(h1t_scr[...], dqkv_scr[j, :, hs])
-        gw_ref[:, wcol(half, 3 * HALF, HALF)] += dot(cott_scr[...], ctx_scr[:, hs])
+        gw_ref[:, wcol(half, QKV * HALF, HALF)] += dot(cott_scr[...], ctx_scr[:, hs])
 
     n = n_scr[...]
     d1, d2 = rnd(dh1_scr[...]), rnd(dh2_scr[...])
-    for i, v in zip((0, 1, 2, 3, 5, 6, 7), (d1 * n, d1, d2 * n, d2, *(dqkv_scr[j].astype(F32) for j in range(3)))):
+    for i, v in zip((0, 1, 2, 3, 5, 6, 7), (d1 * n, d1, d2 * n, d2, *(dqkv_scr[j].astype(F32) for j in range(QKV)))):
         gs_ref[i] += row_sums(v)
     gn = d1 * g1 + d2 * g2
     s_scr[0] = cot.astype(F32) + inv_scr[...] * (
@@ -352,6 +359,8 @@
     def _():
         save = pltpu.make_async_copy(gw_ref, gw_out, init_sem.at[0])
         save.start()
+        gs_out[...] = jnp.sum(gs_ref[...], axis=1)
+        gb1_out[...] = jnp.sum(gb1_ref[...], axis=0, keepdims=True)
         take_peer(step)
         for at in (step - 1, step):
             drain(at)
@@ -363,6 +372,8 @@
             for k in range(1, RING):
                 gx_copy(at, k).wait_recv()
         save.wait()
+        for k in range(RING):
+            id_copy(k).wait()
 
 
 def rope_consts():
@@ -389,14 +400,14 @@
     return pl.pallas_call(
         layer_kernel,
         grid=(count,),
-        in_specs=[seq, own_seq] + [vm] * 4 + [hbm] * (len(args) - 6),
-        out_specs=[hbm] * 4 + [vm] * 2,
-        out_shape=[jax.ShapeDtypeStruct((2 * count, S, D), BF16), jax.ShapeDtypeStruct((RING, count * S, LANES), F32), jax.ShapeDtypeStruct((count, S, D), F32),
-                   jax.ShapeDtypeStruct((D, 2 * WIDE), F32), jax.ShapeDtypeStruct((ROW, ROW, D), F32), jax.ShapeDtypeStruct((ROW, FF), F32)],
-        scratch_shapes=[pltpu.VMEM((D, 2 * WIDE), F32), pltpu.VMEM((3 * S, D), BF16), low(), pltpu.VMEM((D, FF), BF16), pltpu.VMEM((FF, D), BF16)] + [table()] * 4
+        in_specs=[seq, own_seq] + [vm] * 9 + [hbm] * (len(args) - 11),
+        out_specs=[hbm] * 5 + [vm] * 2,
+        out_shape=[jax.ShapeDtypeStruct((2 * count, S, D), BF16), jax.ShapeDtypeStruct((RING, count * S, LANES), F32), jax.ShapeDtypeStruct((count, S, D), F32), jax.ShapeDtypeStruct((RING, count * S // LANES, LANES), jnp.int32),
+                   jax.ShapeDtypeStruct((D, 2 * WIDE), F32), jax.ShapeDtypeStruct((ROW, D), F32), jax.ShapeDtypeStruct((1, FF), F32)],
+        scratch_shapes=[pltpu.VMEM((D, 2 * WIDE), F32), pltpu.VMEM((ROW, ROW, D), F32), pltpu.VMEM((ROW, FF), F32), pltpu.VMEM((QKV * S, D), BF16), low(), pltpu.VMEM((D, FF), BF16), pltpu.VMEM((FF, D), BF16)] + [table()] * 4
         + [pltpu.VMEM((S, 1), F32)] + [low()] * 7 + [low(3)] * 2 + [table(2)] + [low(2)] * 3 + [thin] + [thin_low] * 3 + [small] * 2
         + [table(2), pltpu.VMEM((2, RING, S, LANES), F32), table(2), table(count)] + [low(2)] * 2
-        + [dma((count,)), dma((count,)), dma((2,)), dma((2, RING)), dma((count, RING)), dma((2,)), dma((2,)), dma((count,)), dma((2,)), dma((2,)), dma((16,))],
+        + [dma((count,)), dma((count,)), dma((2,)), dma((RING,)), dma((RING,)), dma((2, RING)), dma((count, RING)), dma((2,)), dma((2,)), dma((count,)), dma((2,)), dma((2,)), dma((16,))],
         compiler_params=pltpu.CompilerParams(dimension_semantics=("arbitrary",), collective_id=1, has_side_effects=True,
                                              vmem_limit_bytes=VMEM_LIMIT),
         cost_estimate=pl.CostEstimate(flops=count * 30_000_000_000, bytes_accessed=60_000_000, transcendentals=0),
@@ -404,7 +415,7 @@
     )(*args)
 
 
-STEPS, UNROLL = 8, 8
+STEPS, UNROLL = 8, 16
 STEP = PAD // STEPS
 
 
@@ -445,10 +456,16 @@
         @pl.loop(0, part // UNROLL)
         def _(g):
             t0 = pl.multiple_of(first + g * UNROLL, UNROLL)
-            for j in range(UNROLL):
+            for j in range(0, UNROLL, 2):
+                pairs = []
                 for a, src in ((acc, k), (acc2, k + 1)):
-                    row = pl.ds(ids_ref[src * count + t0 + j], 1)
-                    a[row, :] += rows_ref[src, pl.ds(t0 + j, 1), :]
+                    i0, i1 = (ids_ref[src * count + t0 + j + d] for d in BOTH)
+                    x0, x1 = (rows_ref[src, pl.ds(t0 + j + d, 1), :] for d in BOTH)
+                    r0, r1 = pl.ds(i0, 1), pl.ds(i1, 1)
+                    pairs.append((a, r0, a[r0, :] + x0, r1, a[r1, :] + (x1 + jnp.where(i0 == i1, x0, 0.0))))
+                for a, r0, v0, r1, v1 in pairs:
+                    a[r0, :] = v0
+                    a[r1, :] = v1
     lo_store(blocks - 1).wait()
     copies = []
     for i in range(2 * STEPS):
@@ -697,13 +714,9 @@
     arg_specs = (P(dp, no), P(tp, no), one, one, one, one, P(no, tp, no, no), P(tp, no, no), P(tp, no, no), one, P(no, tp), P(tp), P(tp, no), one, P(dp, no, no))
     out_specs = (P(dp, no, no), P(tp, dp), vec_dp, vec_dp, vec_dp, vec_dp, P(dp, tp, no, no), both, P(tp, no, dp), vec_dp, P(dp, tp), both, P(tp, dp), vec_dp)
     chips = mesh.shape[dp]
-    plane = chips // RING
 
     def swap(v):
         return lax.ppermute(v, tp, [(0, 1), (1, 0)])
-
-    def z_shift(v, k):
-        return lax.ppermute(v, dp, [(i, (i + k * plane) % chips) for i in range(chips)]) if k else v
 
     def device_step(token_ids, embed_table, ln1_gain, ln1_bias, ln2_gain, ln2_bias, w_qkv, b_qkv, w_dense, b_dense, w_fc1, b_fc1, w_fc2, b_fc2, cotangent):
         core = lax.axis_index(tp)
@@ -711,38 +724,36 @@
         seqs = token_ids.shape[0] // 2
         f = lambda v: v.astype(F32)
 
-        wq_own = w_qkv.transpose(2, 1, 3, 0).reshape(3 * HALF, D)
+        wq_own = w_qkv.transpose(2, 1, 3, 0).reshape(QKV * HALF, D)
         wd_own = w_dense.reshape(HALF, D)
         rows_peer = swap(f(jnp.concatenate([wq_own, wd_own, w_fc2], axis=0)))
         fc1_peer = swap(f(w_fc1))
         wide = FF // 2
         bias = f(jnp.concatenate([jnp.pad(b_qkv.transpose(1, 0, 2).reshape(3, HALF), ((0, 0), (0, wide - HALF))), b_fc1.reshape(1, wide)], axis=0))
         bias_peer = swap(bias)
-        vec = jnp.stack([ln1_gain, ln1_bias, ln2_gain, ln2_bias, b_dense, b_fc2])
 
         tokens = jnp.where(core == 0, token_ids, jnp.roll(token_ids, seqs, axis=0)).reshape(-1)
         local = tokens - core * vocab_local
-        codes = jnp.where((local >= 0) & (local < vocab_local), local, vocab_local)
-        x_send, x_own = look_up_call(codes, embed_table)
-        flat = tokens[:seqs * S]
-        ids = jnp.concatenate([z_shift(flat, k) for k in range(RING)]) - core * vocab_local
-
-        args = (x_own, cotangent, vec, bias, bias_peer, rope_consts(), x_send, wq_own, wd_own, w_fc1, w_fc2, rows_peer, fc1_peer)
-        layer_out, rows, _, grad_w, grad_s, grad_b1 = layer_call(*args)
-
-        dense, layer_out = table_call(jnp.where(ids < 0, ids + 2 * vocab_local, ids), rows, layer_out, vocab_local)
-
-        small = jnp.sum(grad_s, axis=1)
+        row = jnp.where((local >= 0) & (local < vocab_local), local, vocab_local)
+        codes = (row & -ROW) | ((lax.iota(jnp.int32, tokens.size) - row) & (ROW - 1))
+        x_send, x_own = look_up_call(codes, embed_table.reshape(-1, ROW, D))
+        ids = jnp.where(local < 0, local + 2 * vocab_local, local)[:seqs * S].reshape(-1, LANES)
+
+        args = (x_own, cotangent, ln1_gain, ln1_bias, ln2_gain, ln2_bias, b_dense, b_fc2, bias, bias_peer, rope_consts(), x_send, ids, wq_own, wd_own, w_fc1, w_fc2, rows_peer, fc1_peer)
+        layer_out, rows, _, ids, grad_w, small, grad_b1 = layer_call(*args)
+
+        dense, layer_out = table_call(ids.reshape(-1), rows, layer_out, vocab_local)
+
         norms = small[:5].reshape(5, chips, ROW).transpose(1, 0, 2).reshape(chips, 5 * ROW)
         grad_bq = small[5:].reshape(3, 2, PAIRS, HD).transpose(1, 2, 0, 3).reshape(2, chips, -1)
-        grad_bf = jnp.sum(grad_b1, axis=0).reshape(2, chips, -1)
+        grad_bf = grad_b1.reshape(2, chips, -1)
         extra = jnp.concatenate([jnp.stack([norms, norms]), grad_bq, grad_bf], axis=2)
         ends = (5 * ROW, 5 * ROW + grad_bq.shape[2], extra.shape[2])
         extra = jnp.pad(extra[:, :, None, :], ((0, 0), (0, 0), (0, ROW - 1), (0, EXTRA - ends[2])))
         ring3 = (RING,) * 3
         sum_embed, total = tail_call(dense.reshape(2, RING, RING, ROW, PAD), grad_w.reshape(ring3 + (ROW, 2 * WIDE)),
                                      extra.reshape((2,) + ring3 + (ROW, EXTRA)), vocab_local)
-        qkv = 3 * HALF
+        qkv = QKV * HALF
         sum_wqkv = total[:, :qkv].reshape(ROW, 3, PAIRS, HD).transpose(0, 2, 1, 3)
         sum_wdense = total[:, qkv:wide].reshape(ROW, PAIRS, HD).transpose(1, 2, 0)
         sum_wfc1, sum_wfc2 = total[:, wide:2 * wide], total[:, 2 * wide:WIDE].T

time: 405 us -> 389 us (0.960)
  Pallas kernels: 365 us -> 358 us
  starting transfers between devices: 7.24 us -> 0.51 us
    pallas_call x1, Pallas kernels: 57.4 us -> 50.4 us  [table_call(): pl.pallas_call(functools.partial(table_kernel, half), grid_spec=pltpu.Pre...]
    ppermute x3 -> x0, starting transfers between devices: 6.72 us -> none  [z_shift(): lax.ppermute(v, dp, [(i, (i + k * plane) % chips) for i in range(chips)])]
  transfers between devices with their start and end apart: 6 -> 3, of which waited for: 0 -> 0; matrix products, arithmetic and copies ran while one was open for 4% -> 3% of each run, Pallas kernels for 9% -> 8%
where the time goes in v1:
time: 389 us; the launch traced here: 388 us
  Pallas kernels  358 us (92%)
  local copies, waits for them, and re-layouts  17.1 us (4%)
  other arithmetic  10.9 us (3%)
    pallas_call x1, Pallas kernels, layer_call(): pl.pallas_call(layer_kernel, grid=(count,), in_specs=[seq, own_seq] + [vm...  181 us
    pallas_call x1, Pallas kernels, tail_call(): pl.pallas_call(tail_kernel, in_specs=[hbm] * 3, out_specs=[vm] * 2, out_s...  96 us
    pallas_call x1, Pallas kernels, table_call(): pl.pallas_call(functools.partial(table_kernel, half), grid_spec=pltpu.Pre...  50.4 us
    pallas_call x1, Pallas kernels, look_up_call(): pl.pallas_call(look_up_kernel, grid_spec=pltpu.PrefetchScalarGridSpec(num...  30.9 us
  transfers between devices with their start and end apart: 3, of which 0 were waited for; matrix products, arithmetic and copies ran while one was open for 3% of the time, Pallas kernels for 8%

profile of v1, /device:TPU:0, one launch (start us, length us, event | category | flops | bytes accessed | tf_op | source)
XLA Modules:
  0.0 387.5 jit_solution(17731330552603343623)
XLA Ops:
  0.6 0.0 copy-start.1
  0.7 0.9 reshape.379
  1.5 0.7 reshape.380
  2.2 0.6 fusion.15.bo_ref
  2.8 0.0 collective-permute-start
  2.8 1.2 copy.33
  4.0 0.0 copy-start
  4.0 0.0 copy-start.2
  4.1 4.1 %maximum_convert_fusion = f32[2048,512]{1,0:T(8,128)} fusion(bf16[1024,512]{1,0:T(8,128)(2,1)} %to_ref.1, bf16[256,512]{1,0:T(8,128)(2,1)} %bitcast.49, bf16[768,512]{1,0:T(8,128)(2,1)S(1)} %bitcast.42), kind=kLoop, calls=%fused_computation | loop fusion | flops 6291456 | bytes 6291456 | tf_op jit(solution)/shard_map/convert_element_type | solution.py:725
  8.2 0.5 collective-permute-start.1
  8.7 0.0 copy-done.1
  8.7 1.6 convert_element_type.38
  10.2 0.0 copy-done
  10.2 0.0 collective-permute-start.2
  10.2 0.0 copy-done.2
  10.3 0.6 and_or_fusion.codes_ref
  10.9 30.9 %look_up.1 = (f32[8,512,512]{2,1,0:T(8,128)}, bf16[8,512,512]{2,1,0:T(8,128)(2,1)}) custom-call(s32[8192]{0:T(1024)} %and_or_fusion.codes_ref, bf16[3144,8,512]{2,1,0:T(8,128)(2,1)} %bitcast.59), custom_call_target="tpu_custom_call" | custom-call | flops 40000000000 | bytes 40000000 | tf_op jit(solution)/shard_map/look_up/pallas_call | solution.py:86
  41.9 0.6 compare_select_fusion.ids_ref
  42.5 1.0 fusion.1
  43.5 0.9 pad_maximum_fusion.rope_ref
  44.5 0.0 collective-permute-done.bp_ref
  44.5 0.0 collective-permute-done.2.fp_ref
  44.5 0.0 collective-permute-done.1.rp_ref
  44.5 180.8 %layer.1 = (bf16[16,512,512]{2,1,0:T(8,128)(2,1)}, f32[4,4096,128]{2,1,0:T(8,128)}, f32[8,512,512]{2,1,0:T(8,128)}, s32[4,32,128]{2,1,0:T(8,128)}, f32[512,6144]...) custom-call(bf16[8,512,512]{2,1,0:T(8,128)(2,1)} %get-tuple-element.26.xo_ref, bf16[16,512,512]{2,1,0:T(8,128)(2,1)} %cot_ref.1, ...), custom_call_target="tpu_custom_call" | custom-call | flops 240000008192 | bytes 60000000 | tf_op jit(solution)/shard_map/layer/pallas_call | solution.py:400
  225.3 0.5 broadcast.409
  225.8 1.4 reduce.3
  227.2 0.1 reshape.389
  227.3 0.1 copy.37
  227.4 0.7 slice.62
  228.1 0.1 reshape.387
  228.2 0.1 reshape.388
  228.3 0.1 copy.36
  228.4 0.8 reshape.386
  229.2 0.1 copy.34
  229.3 0.1 copy.40
  229.4 0.8 pad.9.clone
  230.3 50.4 %table.1 = (f32[2,128,25600]{2,1,0:T(8,128)}, bf16[16,512,512]{2,1,0:T(8,128)(2,1)}) custom-call(s32[16384]{0:T(1024)} %bitcast.53, f32[4,4096,128]{2,1,0:T(8,128)} %get-tuple-element.29.rows_hbm, bf16[16,512,512]{2,1,0:T(8,128)(2,1)} %get-tuple-element.30.lo_ref), custom_call_target="tpu_custom_call" | custom-call | flops 4000000000 | bytes 34000000 | tf_op jit(solution)/shard_map/table/pallas_call | solution.py:488
  280.7 96.0 %tail.1 = (f32[8,25152]{1,0:T(8,128)}, f32[8,3200]{1,0:T(8,128)}) custom-call(f32[2,4,4,8,25600]{4,3,2,1,0:T(8,128)} %bitcast.40, f32[4,4,4,8,6144]{4,3,2,1,0:T(8,128)} %bitcast.41, f32[2,4,4,4,8,128]{5,4,3,2,1,0:T(8,128)} %bitcast.44), custom_call_target="tpu_custom_call" | custom-call | tf_op jit(solution)/shard_map/tail/pallas_call | solution.py:700
  376.7 1.5 slice_bitcast_fusion.2
  378.2 0.0 copy-start.3
  378.2 0.7 slice.63
  378.9 1.3 slice_bitcast_fusion.3
  380.2 0.7 slice.66
  380.9 1.4 slice_bitcast_fusion
  382.3 1.3 slice_bitcast_fusion.1
  383.5 0.7 reshape.391
  384.2 0.1 reshape.392
  384.3 0.6 copy.44
  384.9 0.5 copy.48
  385.4 2.1 copy.49
  387.5 0.0 copy-done.3
  (8 shorter events, 0.1 us)
Async XLA Ops:
  0.6 8.0 %copy-start.1 = (bf16[512,1024]{1,0:T(8,128)(2,1)S(1)}, bf16[512,1024]{1,0:T(8,128)(2,1)}, u32[]{:S(2)}) copy-start(bf16[512,1024]{1,0:T(8,128)(2,1)} %fo_ref.1) | copy-start | bytes 3145732
  2.8 41.7 %collective-permute-start = (f32[4,1024]{1,0:T(4,128)}, f32[4,1024]{1,0:T(4,128)}, u32[]{:S(2)}, u32[]{:S(2)}) collective-permute-start(f32[4,1024]{1,0:T(4,128)} %fusion.15.bo_ref), channel_id=1, source_target_pairs={{0,64},{64,0},{1,65},{65,1},{2,66},{66,2},{3,67},{67,3},{4,68},{68... | collective-permute-start | bytes 49160 | tf_op jit(solution)/shard_map/ppermute | solution.py:719
  4.0 6.2 %copy-start = (bf16[3,4,64,512]{3,2,1,0:T(8,128)(2,1)}, bf16[3,4,64,512]{3,2,1,0:T(8,128)(2,1)S(1)}, u32[]{:S(2)}) copy-start(bf16[3,4,64,512]{3,2,1,0:T(8,128)(2,1)S(1)} %copy.33) | copy-start | bytes 2359300
  4.0 6.2 %copy-start.2 = (s32[16,512]{1,0:T(8,128)S(1)}, s32[16,512]{1,0:T(8,128)}, u32[]{:S(2)}) copy-start(s32[16,512]{1,0:T(8,128)} %param.15) | copy-start | bytes 98308
  8.2 36.3 %collective-permute-start.1 = (f32[2048,512]{1,0:T(8,128)}, f32[2048,512]{1,0:T(8,128)}, u32[]{:S(2)}, u32[]{:S(2)}) collective-permute-start(f32[2048,512]{1,0:T(8,128)} %maximum_convert_fusion), channel_id=1, source_target_pairs={{0,64},{64,0},{1,65},{65,1},{2,66},{66,2},{3,67},{67,3},{4,68},{68... | collective-permute-start | bytes 12582920 | tf_op jit(solution)/shard_map/ppermute | solution.py:719
  10.2 34.2 %collective-permute-start.2 = (f32[512,1024]{1,0:T(8,128)}, f32[512,1024]{1,0:T(8,128)}, u32[]{:S(2)}, u32[]{:S(2)}) collective-permute-start(f32[512,1024]{1,0:T(8,128)} %convert_element_type.38), channel_id=1, source_target_pairs={{0,64},{64,0},{1,65},{65,1},{2,66},{66,2},{3,67},{67,3},{4,68},{68... | collective-permute-start | bytes 6291464 | tf_op jit(solution)/shard_map/ppermute | solution.py:719
  378.2 9.4 %copy-start.3 = (f32[8]{0:T(128)}, f32[8]{0:T(128)S(1)}, u32[]{:S(2)}) copy-start(f32[8]{0:T(128)S(1)} %get-tuple-element.103) | copy-start | bytes 100

commit v2 on v1

--- a/solution.py
+++ b/solution.py
@@ -95,9 +95,9 @@
     )(codes, table)
 
 
-def layer_kernel(xo_ref, cot_ref, g1_ref, b1_ref, g2_ref, b2_ref, bd_ref, bf_ref, bo_ref, bp_ref, rope_ref, xs_ref, ids_ref, qo_ref, do_ref, fo_ref, to_ref, rp_ref, fp_ref,
+def layer_kernel(xo_ref, cot_ref, g1_ref, b1_ref, g2_ref, b2_ref, bd_ref, bf_ref, bq_ref, bf1_ref, rope_ref, xs_ref, ids_ref, qo_ref, do_ref, fo_ref, to_ref, rp_ref, fp_ref,
                  out_ref, rows_ref, xin_ref, idz_ref, gw_out, gs_out, gb1_out,
-                 gw_ref, gs_ref, gb1_ref, wqkv, wd, w1, w2, n_scr, acc_scr, dh2_scr, dh1_scr, inv_scr, h1_scr, h2_scr, h1t_scr, h2t_scr, cott_scr, dctx_scr, ctx_scr,
+                 bo_scr, bp_scr, gw_ref, gs_ref, gb1_ref, wqkv, wd, w1, w2, n_scr, acc_scr, dh2_scr, dh1_scr, inv_scr, h1_scr, h2_scr, h1t_scr, h2t_scr, cott_scr, dctx_scr, ctx_scr,
                  qkv_scr, dqkv_scr, s_scr, dp_scr, pb_scr, ds_scr, a_scr, du_scr, u_scr, da_scr, dk_scr, dv_scr,
                  xp_buf, gx_buf, out_buf, peer_buf, own_low, peer_low, x_send, x_recv, x_load, id_send, id_recv, gx_send, gx_recv, gx_local, out_send, out_recv, own_sem, peer_sem, init_sem):
     step, last = pl.program_id(0), pl.num_programs(0) - 1
@@ -119,7 +119,7 @@
     def id_copy(k):
         if k:
             return pltpu.make_async_remote_copy(ids_ref, idz_ref.at[k], id_send.at[k], id_recv.at[k], device_id=z_device(k), device_id_type=MESH)
-        return pltpu.make_async_copy(ids_ref, idz_ref.at[k], id_send.at[k])
+        return pltpu.make_async_copy(ids_ref, idz_ref.at[k], id_send.at[RING])
 
     @pl.when(step == 0)
     def _():
@@ -137,6 +137,11 @@
         for dst in (gw_ref, gs_ref, gb1_ref):
             dst[...] = jnp.zeros_like(dst)
         n = FF // 2
+        bo_scr[...] = jnp.zeros_like(bo_scr)
+        bo_scr[QKV:, :] = bf1_ref[...].astype(F32).reshape(1, n)
+        for j in range(QKV):
+            for h in range(RING):
+                bo_scr[j:j + 1, block(h, HD)] = bq_ref[j, h:h + 1, :].astype(F32)
         moves = [(qo_ref.at[block(j, HALF)], wqkv.at[block(2 * j, HALF)]) for j in range(QKV)]
         moves += [(do_ref, wd.at[:HALF]), (to_ref, w2.at[:n]), (fo_ref, w1.at[:, :n])]
         tables = (n_scr, acc_scr, dh2_scr, dh1_scr, s_scr.at[0], s_scr.at[1])
@@ -144,8 +149,11 @@
         copies = [pltpu.make_async_copy(src, dst, init_sem.at[i]) for i, (src, dst) in enumerate(moves + list(zip(parts, tables)))]
         for c in copies:
             c.start()
+        biases = pltpu.make_async_remote_copy(bo_scr, bp_scr, id_send.at[0], id_recv.at[0], device_id=peer, device_id_type=MESH)
         for c in copies:
             c.wait()
+        biases.start()
+        biases.wait()
         for j in range(QKV):
             wqkv[block(2 * j + 1, HALF), :] = tables[j // 2][block(j % 2, HALF), :].astype(BF16)
         wd[HALF:, :] = tables[1][HALF:, :].astype(BF16)
@@ -205,7 +213,7 @@
 
     def bias(row, i, n):
         width = HALF if row < 3 else FF // 2
-        src, i = (bo_ref, i) if i < width // n else (bp_ref, i - width // n)
+        src, i = (bo_scr, i) if i < width // n else (bp_scr, i - width // n)
         return src[row:row + 1, block(i, n)]
 
     dctx_scr[...] = dot(cot, wd[...], NT).astype(BF16)
@@ -360,7 +368,7 @@
         save = pltpu.make_async_copy(gw_ref, gw_out, init_sem.at[0])
         save.start()
         gs_out[...] = jnp.sum(gs_ref[...], axis=1)
-        gb1_out[...] = jnp.sum(gb1_ref[...], axis=0, keepdims=True)
+        gb1_out[...] = jnp.sum(gb1_ref[...], axis=0)
         take_peer(step)
         for at in (step - 1, step):
             drain(at)
@@ -403,11 +411,11 @@
         in_specs=[seq, own_seq] + [vm] * 9 + [hbm] * (len(args) - 11),
         out_specs=[hbm] * 5 + [vm] * 2,
         out_shape=[jax.ShapeDtypeStruct((2 * count, S, D), BF16), jax.ShapeDtypeStruct((RING, count * S, LANES), F32), jax.ShapeDtypeStruct((count, S, D), F32), jax.ShapeDtypeStruct((RING, count * S // LANES, LANES), jnp.int32),
-                   jax.ShapeDtypeStruct((D, 2 * WIDE), F32), jax.ShapeDtypeStruct((ROW, D), F32), jax.ShapeDtypeStruct((1, FF), F32)],
-        scratch_shapes=[pltpu.VMEM((D, 2 * WIDE), F32), pltpu.VMEM((ROW, ROW, D), F32), pltpu.VMEM((ROW, FF), F32), pltpu.VMEM((QKV * S, D), BF16), low(), pltpu.VMEM((D, FF), BF16), pltpu.VMEM((FF, D), BF16)] + [table()] * 4
+                   jax.ShapeDtypeStruct((D, 2 * WIDE), F32), jax.ShapeDtypeStruct((ROW, D), F32), jax.ShapeDtypeStruct((FF,), F32)],
+        scratch_shapes=[pltpu.VMEM((RING, FF // 2), F32)] * 2 + [pltpu.VMEM((D, 2 * WIDE), F32), pltpu.VMEM((ROW, ROW, D), F32), pltpu.VMEM((ROW, FF), F32), pltpu.VMEM((QKV * S, D), BF16), low(), pltpu.VMEM((D, FF), BF16), pltpu.VMEM((FF, D), BF16)] + [table()] * 4
         + [pltpu.VMEM((S, 1), F32)] + [low()] * 7 + [low(3)] * 2 + [table(2)] + [low(2)] * 3 + [thin] + [thin_low] * 3 + [small] * 2
         + [table(2), pltpu.VMEM((2, RING, S, LANES), F32), table(2), table(count)] + [low(2)] * 2
-        + [dma((count,)), dma((count,)), dma((2,)), dma((RING,)), dma((RING,)), dma((2, RING)), dma((count, RING)), dma((2,)), dma((2,)), dma((count,)), dma((2,)), dma((2,)), dma((16,))],
+        + [dma((count,)), dma((count,)), dma((2,)), dma((RING + 1,)), dma((RING,)), dma((2, RING)), dma((count, RING)), dma((2,)), dma((2,)), dma((count,)), dma((2,)), dma((2,)), dma((16,))],
         compiler_params=pltpu.CompilerParams(dimension_semantics=("arbitrary",), collective_id=1, has_side_effects=True,
                                              vmem_limit_bytes=VMEM_LIMIT),
         cost_estimate=pl.CostEstimate(flops=count * 30_000_000_000, bytes_accessed=60_000_000, transcendentals=0),
@@ -708,6 +716,30 @@
     )(t, g, e)
 
 
+def finish_kernel(e_ref, w_ref, oe, o1, o2, oq, od, *small):
+    oe[...] = e_ref[...]
+    wide = RING * HALF
+    for dst, at in ((o1, wide), (o2, 2 * wide)):
+        dst[...] = w_ref[:, at:at + wide]
+    for h in range(RING):
+        for j in range(QKV):
+            oq[:, j, h, :] = w_ref[:, j * HALF + h * HD:j * HALF + (h + 1) * HD]
+        od[h] = w_ref[:, block(QKV * RING + h, HD)]
+    at = WIDE
+    for dst in small:
+        n = dst.shape[0]
+        dst[...] = w_ref[0, at:at + n]
+        at += n
+
+
+def finish_call(e, w, small):
+    shape = jax.ShapeDtypeStruct
+    vm = pl.BlockSpec(memory_space=pltpu.VMEM)
+    outs = [shape(e.shape, F32)] + [shape((ROW, RING * HALF), F32)] * 2 + [shape((ROW, QKV, RING, HD), F32), shape((RING, ROW, HD), F32)]
+    outs += [shape((n,), F32) for n in small]
+    return pl.pallas_call(finish_kernel, in_specs=[vm] * 2, out_specs=[vm] * len(outs), out_shape=outs, name="finish")(e, w)
+
+
 def solution(mesh):
     tp, dp, no = 'tp', 'dp', None
     one, vec_dp, both = P(no), P(dp), P((tp, dp))
@@ -728,9 +760,6 @@
         wd_own = w_dense.reshape(HALF, D)
         rows_peer = swap(f(jnp.concatenate([wq_own, wd_own, w_fc2], axis=0)))
         fc1_peer = swap(f(w_fc1))
-        wide = FF // 2
-        bias = f(jnp.concatenate([jnp.pad(b_qkv.transpose(1, 0, 2).reshape(3, HALF), ((0, 0), (0, wide - HALF))), b_fc1.reshape(1, wide)], axis=0))
-        bias_peer = swap(bias)
 
         tokens = jnp.where(core == 0, token_ids, jnp.roll(token_ids, seqs, axis=0)).reshape(-1)
         local = tokens - core * vocab_local
@@ -739,27 +768,23 @@
         x_send, x_own = look_up_call(codes, embed_table.reshape(-1, ROW, D))
         ids = jnp.where(local < 0, local + 2 * vocab_local, local)[:seqs * S].reshape(-1, LANES)
 
-        args = (x_own, cotangent, ln1_gain, ln1_bias, ln2_gain, ln2_bias, b_dense, b_fc2, bias, bias_peer, rope_consts(), x_send, ids, wq_own, wd_own, w_fc1, w_fc2, rows_peer, fc1_peer)
+        args = (x_own, cotangent, ln1_gain, ln1_bias, ln2_gain, ln2_bias, b_dense, b_fc2, b_qkv.transpose(1, 0, 2), b_fc1, rope_consts(), x_send, ids, wq_own, wd_own, w_fc1, w_fc2, rows_peer, fc1_peer)
         layer_out, rows, _, ids, grad_w, small, grad_b1 = layer_call(*args)
 
         dense, layer_out = table_call(ids.reshape(-1), rows, layer_out, vocab_local)
 
         norms = small[:5].reshape(5, chips, ROW).transpose(1, 0, 2).reshape(chips, 5 * ROW)
+        norms = jnp.concatenate([norms, norms[:, -ROW:]], axis=1)
         grad_bq = small[5:].reshape(3, 2, PAIRS, HD).transpose(1, 2, 0, 3).reshape(2, chips, -1)
         grad_bf = grad_b1.reshape(2, chips, -1)
         extra = jnp.concatenate([jnp.stack([norms, norms]), grad_bq, grad_bf], axis=2)
-        ends = (5 * ROW, 5 * ROW + grad_bq.shape[2], extra.shape[2])
-        extra = jnp.pad(extra[:, :, None, :], ((0, 0), (0, 0), (0, ROW - 1), (0, EXTRA - ends[2])))
+        extra = jnp.pad(extra[:, :, None, :], ((0, 0), (0, 0), (0, ROW - 1), (0, EXTRA - extra.shape[2])))
         ring3 = (RING,) * 3
         sum_embed, total = tail_call(dense.reshape(2, RING, RING, ROW, PAD), grad_w.reshape(ring3 + (ROW, 2 * WIDE)),
                                      extra.reshape((2,) + ring3 + (ROW, EXTRA)), vocab_local)
-        qkv = QKV * HALF
-        sum_wqkv = total[:, :qkv].reshape(ROW, 3, PAIRS, HD).transpose(0, 2, 1, 3)
-        sum_wdense = total[:, qkv:wide].reshape(ROW, PAIRS, HD).transpose(1, 2, 0)
-        sum_wfc1, sum_wfc2 = total[:, wide:2 * wide], total[:, 2 * wide:WIDE].T
-        last = total[0, WIDE:]
-        n1g, n1b, n2g, n2b, bias = last[:ends[0]].reshape(5, ROW)
-        return (layer_out, sum_embed.T, n1g, n1b, n2g, n2b, sum_wqkv, last[ends[0]:ends[1]], sum_wdense, bias, sum_wfc1,
-                last[ends[1]:ends[2]], sum_wfc2, bias)
+        small = [ROW] * 6 + [grad_bq.shape[2], grad_bf.shape[2]]
+        sum_embed, sum_wfc1, sum_wfc2, sum_wqkv, sum_wdense, n1g, n1b, n2g, n2b, bias, bias2, bq, bf1 = finish_call(sum_embed, total, small)
+        return (layer_out, sum_embed.T, n1g, n1b, n2g, n2b, sum_wqkv.transpose(0, 2, 1, 3), bq, sum_wdense.transpose(0, 2, 1), bias, sum_wfc1,
+                bf1, sum_wfc2.T, bias2)
 
     return jax.shard_map(device_step, mesh=mesh, in_specs=arg_specs, out_specs=out_specs, check_vma=False)

time: 389 us -> 387 us (level)
  local copies, waits for them, and re-layouts: 17.1 us -> 5.03 us
  Pallas kernels: 358 us -> 370 us
    pallas_call x1, Pallas kernels: 181 us -> 191 us  [layer_call(): pl.pallas_call(layer_kernel, grid=(count,), in_specs=[seq, own_seq] + [vm...]
    slice x4 -> x1, local copies, waits for them, and re-layouts: 3.96 us -> 0.01 us  [device_step(): norms = jnp.concatenate([norms, norms[:, -ROW:]], axis=1)]
  transfers between devices with their start and end apart: 3 -> 2, of which waited for: 0 -> 0; matrix products, arithmetic and copies ran while one was open for 3% -> 1% of each run, Pallas kernels for 8% -> 8%
where the time goes in v2:
time: 387 us; the launch traced here: 386 us
  Pallas kernels  370 us (96%)
  other arithmetic  8.91 us (2%)
  local copies, waits for them, and re-layouts  5.03 us (1%)
    pallas_call x1, Pallas kernels, layer_call(): pl.pallas_call(layer_kernel, grid=(count,), in_specs=[seq, own_seq] + [vm...  191 us
    pallas_call x1, Pallas kernels, tail_call(): pl.pallas_call(tail_kernel, in_specs=[hbm] * 3, out_specs=[vm] * 2, out_s...  96 us
    pallas_call x1, Pallas kernels, table_call(): pl.pallas_call(functools.partial(table_kernel, half), grid_spec=pltpu.Pre...  50.4 us
    pallas_call x1, Pallas kernels, look_up_call(): pl.pallas_call(look_up_kernel, grid_spec=pltpu.PrefetchScalarGridSpec(num...  30.9 us
  transfers between devices with their start and end apart: 2, of which 0 were waited for; matrix products, arithmetic and copies ran while one was open for 1% of the time, Pallas kernels for 8%

profile of v2, /device:TPU:0, one launch (start us, length us, event | category | flops | bytes accessed | tf_op | source)
XLA Modules:
  0.0 385.8 jit_solution(1872015507789786201)
XLA Ops:
  0.6 0.0 copy-start.1
  0.7 1.3 copy.32
  2.0 0.0 copy-start
  2.0 0.0 copy-start.2
  2.0 4.1 %maximum_convert_fusion = f32[2048,512]{1,0:T(8,128)} fusion(bf16[1024,512]{1,0:T(8,128)(2,1)} %to_ref.1, bf16[256,512]{1,0:T(8,128)(2,1)} %bitcast.33, bf16[768,512]{1,0:T(8,128)(2,1)S(1)} %bitcast.27), kind=kLoop, calls=%fused_computation | loop fusion | flops 6291456 | bytes 6291456 | tf_op jit(solution)/shard_map/convert_element_type | solution.py:757
  6.1 0.0 collective-permute-start
  6.1 0.0 copy-done.1
  6.1 1.6 convert_element_type.32
  7.7 0.0 copy-done
  7.7 0.5 collective-permute-start.1
  8.2 0.0 copy-done.2
  8.2 1.0 fusion.1
  9.3 0.9 pad_maximum_fusion.rope_ref
  10.2 0.6 compare_select_fusion.ids_ref
  10.8 0.6 and_or_fusion.codes_ref
  11.4 30.9 %look_up.1 = (f32[8,512,512]{2,1,0:T(8,128)}, bf16[8,512,512]{2,1,0:T(8,128)(2,1)}) custom-call(s32[8192]{0:T(1024)} %and_or_fusion.codes_ref, bf16[3144,8,512]{2,1,0:T(8,128)(2,1)} %bitcast.41), custom_call_target="tpu_custom_call" | custom-call | flops 40000000000 | bytes 40000000 | tf_op jit(solution)/shard_map/look_up/pallas_call | solution.py:86
  42.4 0.0 collective-permute-done.1.fp_ref
  42.4 0.0 collective-permute-done.rp_ref
  42.4 190.8 %layer.1 = (bf16[16,512,512]{2,1,0:T(8,128)(2,1)}, f32[4,4096,128]{2,1,0:T(8,128)}, f32[8,512,512]{2,1,0:T(8,128)}, s32[4,32,128]{2,1,0:T(8,128)}, f32[512,6144]...) custom-call(bf16[8,512,512]{2,1,0:T(8,128)(2,1)} %get-tuple-element.39.xo_ref, bf16[16,512,512]{2,1,0:T(8,128)(2,1)} %cot_ref.1, ...), custom_call_target="tpu_custom_call" | custom-call | flops 240000008192 | bytes 60000000 | tf_op jit(solution)/shard_map/layer/pallas_call | solution.py:408
  233.3 0.8 reshape.364
  234.0 0.1 copy.36
  234.1 0.7 slice.26
  234.8 0.1 reshape.362
  234.9 0.1 reshape.363
  235.0 0.1 copy.35
  235.1 0.8 reshape.360
  236.0 0.1 copy.33
  236.1 0.1 copy.38
  236.2 0.8 pad.4.clone
  237.0 50.4 %table.1 = (f32[2,128,25600]{2,1,0:T(8,128)}, bf16[16,512,512]{2,1,0:T(8,128)(2,1)}) custom-call(s32[16384]{0:T(1024)} %bitcast.38, f32[4,4096,128]{2,1,0:T(8,128)} %get-tuple-element.42.rows_hbm, bf16[16,512,512]{2,1,0:T(8,128)(2,1)} %get-tuple-element.43.lo_ref), custom_call_target="tpu_custom_call" | custom-call | flops 4000000000 | bytes 34000000 | tf_op jit(solution)/shard_map/table/pallas_call | solution.py:496
  287.5 96.0 %tail.1 = (f32[8,25152]{1,0:T(8,128)}, f32[8,3200]{1,0:T(8,128)}) custom-call(f32[2,4,4,8,25600]{4,3,2,1,0:T(8,128)} %bitcast.25, f32[4,4,4,8,6144]{4,3,2,1,0:T(8,128)} %bitcast.26, f32[2,4,4,4,8,128]{5,4,3,2,1,0:T(8,128)} %bitcast.29), custom_call_target="tpu_custom_call" | custom-call | tf_op jit(solution)/shard_map/tail/pallas_call | solution.py:708
  383.5 2.2 finish.1
  (10 shorter events, 0.1 us)
Async XLA Ops:
  0.6 5.4 %copy-start.1 = (bf16[512,1024]{1,0:T(8,128)(2,1)S(1)}, bf16[512,1024]{1,0:T(8,128)(2,1)}, u32[]{:S(2)}) copy-start(bf16[512,1024]{1,0:T(8,128)(2,1)} %fo_ref.1) | copy-start | bytes 3145732
  2.0 5.7 %copy-start = (bf16[3,4,64,512]{3,2,1,0:T(8,128)(2,1)}, bf16[3,4,64,512]{3,2,1,0:T(8,128)(2,1)S(1)}, u32[]{:S(2)}) copy-start(bf16[3,4,64,512]{3,2,1,0:T(8,128)(2,1)S(1)} %copy.32) | copy-start | bytes 2359300
  2.0 6.2 %copy-start.2 = (s32[16,512]{1,0:T(8,128)S(1)}, s32[16,512]{1,0:T(8,128)}, u32[]{:S(2)}) copy-start(s32[16,512]{1,0:T(8,128)} %param.15) | copy-start | bytes 98308
  6.1 36.3 %collective-permute-start = (f32[2048,512]{1,0:T(8,128)}, f32[2048,512]{1,0:T(8,128)}, u32[]{:S(2)}, u32[]{:S(2)}) collective-permute-start(f32[2048,512]{1,0:T(8,128)} %maximum_convert_fusion), channel_id=1, source_target_pairs={{0,64},{64,0},{1,65},{65,1},{2,66},{66,2},{3,67},{67,3},{4,68},{68... | collective-permute-start | bytes 12582920 | tf_op jit(solution)/shard_map/ppermute | solution.py:751
  7.7 34.7 %collective-permute-start.1 = (f32[512,1024]{1,0:T(8,128)}, f32[512,1024]{1,0:T(8,128)}, u32[]{:S(2)}, u32[]{:S(2)}) collective-permute-start(f32[512,1024]{1,0:T(8,128)} %convert_element_type.32), channel_id=1, source_target_pairs={{0,64},{64,0},{1,65},{65,1},{2,66},{66,2},{3,67},{67,3},{4,68},{68... | collective-permute-start | bytes 6291464 | tf_op jit(solution)/shard_map/ppermute | solution.py:751

commit v3 on v2

--- a/solution.py
+++ b/solution.py
@@ -95,9 +95,9 @@
     )(codes, table)
 
 
-def layer_kernel(xo_ref, cot_ref, g1_ref, b1_ref, g2_ref, b2_ref, bd_ref, bf_ref, bq_ref, bf1_ref, rope_ref, xs_ref, ids_ref, qo_ref, do_ref, fo_ref, to_ref, rp_ref, fp_ref,
+def layer_kernel(xo_ref, cot_ref, g1_ref, b1_ref, g2_ref, b2_ref, bd_ref, bf_ref, bo_ref, bp_ref, rope_ref, xs_ref, ids_ref, qo_ref, do_ref, fo_ref, to_ref, rp_ref, fp_ref,
                  out_ref, rows_ref, xin_ref, idz_ref, gw_out, gs_out, gb1_out,
-                 bo_scr, bp_scr, gw_ref, gs_ref, gb1_ref, wqkv, wd, w1, w2, n_scr, acc_scr, dh2_scr, dh1_scr, inv_scr, h1_scr, h2_scr, h1t_scr, h2t_scr, cott_scr, dctx_scr, ctx_scr,
+                 gw_ref, gs_ref, gb1_ref, wqkv, wd, w1, w2, n_scr, acc_scr, dh2_scr, dh1_scr, inv_scr, h1_scr, h2_scr, h1t_scr, h2t_scr, cott_scr, dctx_scr, ctx_scr,
                  qkv_scr, dqkv_scr, s_scr, dp_scr, pb_scr, ds_scr, a_scr, du_scr, u_scr, da_scr, dk_scr, dv_scr,
                  xp_buf, gx_buf, out_buf, peer_buf, own_low, peer_low, x_send, x_recv, x_load, id_send, id_recv, gx_send, gx_recv, gx_local, out_send, out_recv, own_sem, peer_sem, init_sem):
     step, last = pl.program_id(0), pl.num_programs(0) - 1
@@ -119,7 +119,7 @@
     def id_copy(k):
         if k:
             return pltpu.make_async_remote_copy(ids_ref, idz_ref.at[k], id_send.at[k], id_recv.at[k], device_id=z_device(k), device_id_type=MESH)
-        return pltpu.make_async_copy(ids_ref, idz_ref.at[k], id_send.at[RING])
+        return pltpu.make_async_copy(ids_ref, idz_ref.at[k], id_send.at[k])
 
     @pl.when(step == 0)
     def _():
@@ -137,11 +137,6 @@
         for dst in (gw_ref, gs_ref, gb1_ref):
             dst[...] = jnp.zeros_like(dst)
         n = FF // 2
-        bo_scr[...] = jnp.zeros_like(bo_scr)
-        bo_scr[QKV:, :] = bf1_ref[...].astype(F32).reshape(1, n)
-        for j in range(QKV):
-            for h in range(RING):
-                bo_scr[j:j + 1, block(h, HD)] = bq_ref[j, h:h + 1, :].astype(F32)
         moves = [(qo_ref.at[block(j, HALF)], wqkv.at[block(2 * j, HALF)]) for j in range(QKV)]
         moves += [(do_ref, wd.at[:HALF]), (to_ref, w2.at[:n]), (fo_ref, w1.at[:, :n])]
         tables = (n_scr, acc_scr, dh2_scr, dh1_scr, s_scr.at[0], s_scr.at[1])
@@ -149,11 +144,8 @@
         copies = [pltpu.make_async_copy(src, dst, init_sem.at[i]) for i, (src, dst) in enumerate(moves + list(zip(parts, tables)))]
         for c in copies:
             c.start()
-        biases = pltpu.make_async_remote_copy(bo_scr, bp_scr, id_send.at[0], id_recv.at[0], device_id=peer, device_id_type=MESH)
         for c in copies:
             c.wait()
-        biases.start()
-        biases.wait()
         for j in range(QKV):
             wqkv[block(2 * j + 1, HALF), :] = tables[j // 2][block(j % 2, HALF), :].astype(BF16)
         wd[HALF:, :] = tables[1][HALF:, :].astype(BF16)
@@ -213,7 +205,7 @@
 
     def bias(row, i, n):
         width = HALF if row < 3 else FF // 2
-        src, i = (bo_scr, i) if i < width // n else (bp_scr, i - width // n)
+        src, i = (bo_ref, i) if i < width // n else (bp_ref, i - width // n)
         return src[row:row + 1, block(i, n)]
 
     dctx_scr[...] = dot(cot, wd[...], NT).astype(BF16)
@@ -368,7 +360,7 @@
         save = pltpu.make_async_copy(gw_ref, gw_out, init_sem.at[0])
         save.start()
         gs_out[...] = jnp.sum(gs_ref[...], axis=1)
-        gb1_out[...] = jnp.sum(gb1_ref[...], axis=0)
+        gb1_out[...] = jnp.sum(gb1_ref[...], axis=0, keepdims=True)
         take_peer(step)
         for at in (step - 1, step):
             drain(at)
@@ -411,11 +403,11 @@
         in_specs=[seq, own_seq] + [vm] * 9 + [hbm] * (len(args) - 11),
         out_specs=[hbm] * 5 + [vm] * 2,
         out_shape=[jax.ShapeDtypeStruct((2 * count, S, D), BF16), jax.ShapeDtypeStruct((RING, count * S, LANES), F32), jax.ShapeDtypeStruct((count, S, D), F32), jax.ShapeDtypeStruct((RING, count * S // LANES, LANES), jnp.int32),
-                   jax.ShapeDtypeStruct((D, 2 * WIDE), F32), jax.ShapeDtypeStruct((ROW, D), F32), jax.ShapeDtypeStruct((FF,), F32)],
-        scratch_shapes=[pltpu.VMEM((RING, FF // 2), F32)] * 2 + [pltpu.VMEM((D, 2 * WIDE), F32), pltpu.VMEM((ROW, ROW, D), F32), pltpu.VMEM((ROW, FF), F32), pltpu.VMEM((QKV * S, D), BF16), low(), pltpu.VMEM((D, FF), BF16), pltpu.VMEM((FF, D), BF16)] + [table()] * 4
+                   jax.ShapeDtypeStruct((D, 2 * WIDE), F32), jax.ShapeDtypeStruct((ROW, D), F32), jax.ShapeDtypeStruct((1, FF), F32)],
+        scratch_shapes=[pltpu.VMEM((D, 2 * WIDE), F32), pltpu.VMEM((ROW, ROW, D), F32), pltpu.VMEM((ROW, FF), F32), pltpu.VMEM((QKV * S, D), BF16), low(), pltpu.VMEM((D, FF), BF16), pltpu.VMEM((FF, D), BF16)] + [table()] * 4
         + [pltpu.VMEM((S, 1), F32)] + [low()] * 7 + [low(3)] * 2 + [table(2)] + [low(2)] * 3 + [thin] + [thin_low] * 3 + [small] * 2
         + [table(2), pltpu.VMEM((2, RING, S, LANES), F32), table(2), table(count)] + [low(2)] * 2
-        + [dma((count,)), dma((count,)), dma((2,)), dma((RING + 1,)), dma((RING,)), dma((2, RING)), dma((count, RING)), dma((2,)), dma((2,)), dma((count,)), dma((2,)), dma((2,)), dma((16,))],
+        + [dma((count,)), dma((count,)), dma((2,)), dma((RING,)), dma((RING,)), dma((2, RING)), dma((count, RING)), dma((2,)), dma((2,)), dma((count,)), dma((2,)), dma((2,)), dma((16,))],
         compiler_params=pltpu.CompilerParams(dimension_semantics=("arbitrary",), collective_id=1, has_side_effects=True,
                                              vmem_limit_bytes=VMEM_LIMIT),
         cost_estimate=pl.CostEstimate(flops=count * 30_000_000_000, bytes_accessed=60_000_000, transcendentals=0),
@@ -760,6 +752,9 @@
         wd_own = w_dense.reshape(HALF, D)
         rows_peer = swap(f(jnp.concatenate([wq_own, wd_own, w_fc2], axis=0)))
         fc1_peer = swap(f(w_fc1))
+        wide = FF // 2
+        bias = f(jnp.concatenate([jnp.pad(b_qkv.transpose(1, 0, 2).reshape(3, HALF), ((0, 0), (0, wide - HALF))), b_fc1.reshape(1, wide)], axis=0))
+        bias_peer = swap(bias)
 
         tokens = jnp.where(core == 0, token_ids, jnp.roll(token_ids, seqs, axis=0)).reshape(-1)
         local = tokens - core * vocab_local
@@ -768,7 +763,7 @@
         x_send, x_own = look_up_call(codes, embed_table.reshape(-1, ROW, D))
         ids = jnp.where(local < 0, local + 2 * vocab_local, local)[:seqs * S].reshape(-1, LANES)
 
-        args = (x_own, cotangent, ln1_gain, ln1_bias, ln2_gain, ln2_bias, b_dense, b_fc2, b_qkv.transpose(1, 0, 2), b_fc1, rope_consts(), x_send, ids, wq_own, wd_own, w_fc1, w_fc2, rows_peer, fc1_peer)
+        args = (x_own, cotangent, ln1_gain, ln1_bias, ln2_gain, ln2_bias, b_dense, b_fc2, bias, bias_peer, rope_consts(), x_send, ids, wq_own, wd_own, w_fc1, w_fc2, rows_peer, fc1_peer)
         layer_out, rows, _, ids, grad_w, small, grad_b1 = layer_call(*args)
 
         dense, layer_out = table_call(ids.reshape(-1), rows, layer_out, vocab_local)

time: 387 us -> 380 us (0.982)
  Pallas kernels: 370 us -> 360 us
    pallas_call x1, Pallas kernels: 191 us -> 181 us  [layer_call(): pl.pallas_call(layer_kernel, grid=(count,), in_specs=[seq, own_seq] + [vm...]
  transfers between devices with their start and end apart: 2 -> 3, of which waited for: 0 -> 0; matrix products, arithmetic and copies ran while one was open for 1% -> 3% of each run, Pallas kernels for 8% -> 8%
where the time goes in v3:
time: 380 us; the launch traced here: 379 us
  Pallas kernels  360 us (95%)
  other arithmetic  10.9 us (3%)
  local copies, waits for them, and re-layouts  6.3 us (2%)
    pallas_call x1, Pallas kernels, layer_call(): pl.pallas_call(layer_kernel, grid=(count,), in_specs=[seq, own_seq] + [vm...  181 us
    pallas_call x1, Pallas kernels, tail_call(): pl.pallas_call(tail_kernel, in_specs=[hbm] * 3, out_specs=[vm] * 2, out_s...  96 us
    pallas_call x1, Pallas kernels, table_call(): pl.pallas_call(functools.partial(table_kernel, half), grid_spec=pltpu.Pre...  50.3 us
    pallas_call x1, Pallas kernels, look_up_call(): pl.pallas_call(look_up_kernel, grid_spec=pltpu.PrefetchScalarGridSpec(num...  30.9 us
  transfers between devices with their start and end apart: 3, of which 0 were waited for; matrix products, arithmetic and copies ran while one was open for 3% of the time, Pallas kernels for 8%

profile of v3, /device:TPU:0, one launch (start us, length us, event | category | flops | bytes accessed | tf_op | source)
XLA Modules:
  0.0 378.9 jit_solution(14033791434701831262)
XLA Ops:
  0.6 0.0 copy-start.1
  0.7 0.9 reshape.361
  1.5 0.7 reshape.362
  2.2 0.6 fusion.15.bo_ref
  2.8 0.0 collective-permute-start
  2.8 1.2 copy.32
  4.0 0.0 copy-start
  4.0 0.0 copy-start.2
  4.1 4.1 %maximum_convert_fusion = f32[2048,512]{1,0:T(8,128)} fusion(bf16[1024,512]{1,0:T(8,128)(2,1)} %to_ref.1, bf16[256,512]{1,0:T(8,128)(2,1)} %bitcast.33, bf16[768,512]{1,0:T(8,128)(2,1)S(1)} %bitcast.27), kind=kLoop, calls=%fused_computation | loop fusion | flops 6291456 | bytes 6291456 | tf_op jit(solution)/shard_map/convert_element_type | solution.py:749
  8.2 0.5 collective-permute-start.1
  8.7 0.0 copy-done.1
  8.7 1.6 convert_element_type.38
  10.2 0.0 copy-done
  10.2 0.0 collective-permute-start.2
  10.3 0.0 copy-done.2
  10.3 0.6 and_or_fusion.codes_ref
  10.9 30.9 %look_up.1 = (f32[8,512,512]{2,1,0:T(8,128)}, bf16[8,512,512]{2,1,0:T(8,128)(2,1)}) custom-call(s32[8192]{0:T(1024)} %and_or_fusion.codes_ref, bf16[3144,8,512]{2,1,0:T(8,128)(2,1)} %bitcast.42), custom_call_target="tpu_custom_call" | custom-call | flops 40000000000 | bytes 40000000 | tf_op jit(solution)/shard_map/look_up/pallas_call | solution.py:86
  41.9 0.6 compare_select_fusion.ids_ref
  42.5 1.0 fusion.1
  43.5 0.9 pad_maximum_fusion.rope_ref
  44.5 0.0 collective-permute-done.bp_ref
  44.5 0.0 collective-permute-done.2.fp_ref
  44.5 0.0 collective-permute-done.1.rp_ref
  44.5 180.8 %layer.1 = (bf16[16,512,512]{2,1,0:T(8,128)(2,1)}, f32[4,4096,128]{2,1,0:T(8,128)}, f32[8,512,512]{2,1,0:T(8,128)}, s32[4,32,128]{2,1,0:T(8,128)}, f32[512,6144]...) custom-call(bf16[8,512,512]{2,1,0:T(8,128)(2,1)} %get-tuple-element.39.xo_ref, bf16[16,512,512]{2,1,0:T(8,128)(2,1)} %cot_ref.1, ...), custom_call_target="tpu_custom_call" | custom-call | flops 240000008192 | bytes 60000000 | tf_op jit(solution)/shard_map/layer/pallas_call | solution.py:400
  225.3 0.5 broadcast.409
  225.8 1.4 reduce.3
  227.2 0.1 reshape.372
  227.3 0.1 copy.36
  227.4 0.7 slice.26
  228.1 0.1 reshape.370
  228.2 0.1 reshape.371
  228.3 0.1 copy.35
  228.4 0.8 reshape.368
  229.2 0.1 copy.33
  229.3 0.1 copy.38
  229.4 0.8 pad.9.clone
  230.3 50.3 %table.1 = (f32[2,128,25600]{2,1,0:T(8,128)}, bf16[16,512,512]{2,1,0:T(8,128)(2,1)}) custom-call(s32[16384]{0:T(1024)} %bitcast.38, f32[4,4096,128]{2,1,0:T(8,128)} %get-tuple-element.42.rows_hbm, bf16[16,512,512]{2,1,0:T(8,128)(2,1)} %get-tuple-element.43.lo_ref), custom_call_target="tpu_custom_call" | custom-call | flops 4000000000 | bytes 34000000 | tf_op jit(solution)/shard_map/table/pallas_call | solution.py:488
  280.6 96.0 %tail.1 = (f32[8,25152]{1,0:T(8,128)}, f32[8,3200]{1,0:T(8,128)}) custom-call(f32[2,4,4,8,25600]{4,3,2,1,0:T(8,128)} %bitcast.25, f32[4,4,4,8,6144]{4,3,2,1,0:T(8,128)} %bitcast.26, f32[2,4,4,4,8,128]{5,4,3,2,1,0:T(8,128)} %bitcast.29), custom_call_target="tpu_custom_call" | custom-call | tf_op jit(solution)/shard_map/tail/pallas_call | solution.py:700
  376.6 2.2 finish.1
  (10 shorter events, 0.1 us)
Async XLA Ops:
  0.6 8.0 %copy-start.1 = (bf16[512,1024]{1,0:T(8,128)(2,1)S(1)}, bf16[512,1024]{1,0:T(8,128)(2,1)}, u32[]{:S(2)}) copy-start(bf16[512,1024]{1,0:T(8,128)(2,1)} %fo_ref.1) | copy-start | bytes 3145732
  2.8 41.7 %collective-permute-start = (f32[4,1024]{1,0:T(4,128)}, f32[4,1024]{1,0:T(4,128)}, u32[]{:S(2)}, u32[]{:S(2)}) collective-permute-start(f32[4,1024]{1,0:T(4,128)} %fusion.15.bo_ref), channel_id=1, source_target_pairs={{0,64},{64,0},{1,65},{65,1},{2,66},{66,2},{3,67},{67,3},{4,68},{68... | collective-permute-start | bytes 49160 | tf_op jit(solution)/shard_map/ppermute | solution.py:743
  4.0 6.2 %copy-start = (bf16[3,4,64,512]{3,2,1,0:T(8,128)(2,1)}, bf16[3,4,64,512]{3,2,1,0:T(8,128)(2,1)S(1)}, u32[]{:S(2)}) copy-start(bf16[3,4,64,512]{3,2,1,0:T(8,128)(2,1)S(1)} %copy.32) | copy-start | bytes 2359300
  4.0 6.2 %copy-start.2 = (s32[16,512]{1,0:T(8,128)S(1)}, s32[16,512]{1,0:T(8,128)}, u32[]{:S(2)}) copy-start(s32[16,512]{1,0:T(8,128)} %param.15) | copy-start | bytes 98308
  8.2 36.3 %collective-permute-start.1 = (f32[2048,512]{1,0:T(8,128)}, f32[2048,512]{1,0:T(8,128)}, u32[]{:S(2)}, u32[]{:S(2)}) collective-permute-start(f32[2048,512]{1,0:T(8,128)} %maximum_convert_fusion), channel_id=1, source_target_pairs={{0,64},{64,0},{1,65},{65,1},{2,66},{66,2},{3,67},{67,3},{4,68},{68... | collective-permute-start | bytes 12582920 | tf_op jit(solution)/shard_map/ppermute | solution.py:743
  10.2 34.2 %collective-permute-start.2 = (f32[512,1024]{1,0:T(8,128)}, f32[512,1024]{1,0:T(8,128)}, u32[]{:S(2)}, u32[]{:S(2)}) collective-permute-start(f32[512,1024]{1,0:T(8,128)} %convert_element_type.38), channel_id=1, source_target_pairs={{0,64},{64,0},{1,65},{65,1},{2,66},{66,2},{3,67},{67,3},{4,68},{68... | collective-permute-start | bytes 6291464 | tf_op jit(solution)/shard_map/ppermute | solution.py:743

commit v4 on v3

--- a/solution.py
+++ b/solution.py
@@ -74,7 +74,7 @@
         return got
 
     for k, dst in enumerate((own_ref, peer_ref)):
-        @pl.loop(0, S // ROW, unroll=2)
+        @pl.loop(0, S // ROW, unroll=8)
         def _(g):
             t0 = pl.multiple_of(g * ROW, ROW)
             dst[0, pl.ds(t0, ROW), :] = look_up(k * half + step * S + t0).astype(dst.dtype)
@@ -415,7 +415,7 @@
     )(*args)
 
 
-STEPS, UNROLL = 8, 16
+STEPS, UNROLL = 8, 32
 STEP = PAD // STEPS
 
 
@@ -473,7 +473,7 @@
         if i > 1:
             copies[i - 2].wait()
 
-        @pl.loop(0, STEP // LANES, unroll=5)
+        @pl.loop(0, STEP // LANES, unroll=True)
         def _(b):
             at = pl.ds(pl.multiple_of(h * half + c * STEP + b * LANES, ROW), LANES)
             stage[slot, :, pl.ds(pl.multiple_of(b * LANES, LANES), LANES)] = (acc[at, :] + acc2[at, :]).T

time: 380 us -> 374 us (0.984)
  Pallas kernels: 360 us -> 354 us
    pallas_call x1, Pallas kernels: 50.3 us -> 46.2 us  [table_call(): pl.pallas_call(functools.partial(table_kernel, half), grid_spec=pltpu.Pre...]
where the time goes in v4:
time: 374 us; the launch traced here: 373 us
  Pallas kernels  354 us (95%)
  other arithmetic  10.9 us (3%)
  local copies, waits for them, and re-layouts  6.3 us (2%)
    pallas_call x1, Pallas kernels, layer_call(): pl.pallas_call(layer_kernel, grid=(count,), in_specs=[seq, own_seq] + [vm...  181 us
    pallas_call x1, Pallas kernels, tail_call(): pl.pallas_call(tail_kernel, in_specs=[hbm] * 3, out_specs=[vm] * 2, out_s...  96 us
    pallas_call x1, Pallas kernels, table_call(): pl.pallas_call(functools.partial(table_kernel, half), grid_spec=pltpu.Pre...  46.2 us
    pallas_call x1, Pallas kernels, look_up_call(): pl.pallas_call(look_up_kernel, grid_spec=pltpu.PrefetchScalarGridSpec(num...  28.9 us
  transfers between devices with their start and end apart: 3, of which 0 were waited for; matrix products, arithmetic and copies ran while one was open for 3% of the time, Pallas kernels for 8%

profile of v4, /device:TPU:0, one launch (start us, length us, event | category | flops | bytes accessed | tf_op | source)
XLA Modules:
  0.0 372.7 jit_solution(8742003553088740869)
XLA Ops:
  0.6 0.0 copy-start.1
  0.7 0.9 reshape.361
  1.5 0.7 reshape.362
  2.2 0.6 fusion.15.bo_ref
  2.8 0.0 collective-permute-start
  2.8 1.2 copy.32
  4.0 0.0 copy-start
  4.0 0.0 copy-start.2
  4.1 4.1 %maximum_convert_fusion = f32[2048,512]{1,0:T(8,128)} fusion(bf16[1024,512]{1,0:T(8,128)(2,1)} %to_ref.1, bf16[256,512]{1,0:T(8,128)(2,1)} %bitcast.33, bf16[768,512]{1,0:T(8,128)(2,1)S(1)} %bitcast.27), kind=kLoop, calls=%fused_computation | loop fusion | flops 6291456 | bytes 6291456 | tf_op jit(solution)/shard_map/convert_element_type | solution.py:749
  8.2 0.5 collective-permute-start.1
  8.7 0.0 copy-done.1
  8.7 1.6 convert_element_type.38
  10.2 0.0 copy-done
  10.2 0.0 collective-permute-start.2
  10.3 0.0 copy-done.2
  10.3 0.6 and_or_fusion.codes_ref
  10.9 28.9 %look_up.1 = (f32[8,512,512]{2,1,0:T(8,128)}, bf16[8,512,512]{2,1,0:T(8,128)(2,1)}) custom-call(s32[8192]{0:T(1024)} %and_or_fusion.codes_ref, bf16[3144,8,512]{2,1,0:T(8,128)(2,1)} %bitcast.42), custom_call_target="tpu_custom_call" | custom-call | flops 40000000000 | bytes 40000000 | tf_op jit(solution)/shard_map/look_up/pallas_call | solution.py:86
  39.8 0.6 compare_select_fusion.ids_ref
  40.4 1.0 fusion.1
  41.5 0.9 pad_maximum_fusion.rope_ref
  42.4 0.0 collective-permute-done.bp_ref
  42.4 0.0 collective-permute-done.2.fp_ref
  42.4 0.0 collective-permute-done.1.rp_ref
  42.4 180.8 %layer.1 = (bf16[16,512,512]{2,1,0:T(8,128)(2,1)}, f32[4,4096,128]{2,1,0:T(8,128)}, f32[8,512,512]{2,1,0:T(8,128)}, s32[4,32,128]{2,1,0:T(8,128)}, f32[512,6144]...) custom-call(bf16[8,512,512]{2,1,0:T(8,128)(2,1)} %get-tuple-element.39.xo_ref, bf16[16,512,512]{2,1,0:T(8,128)(2,1)} %cot_ref.1, ...), custom_call_target="tpu_custom_call" | custom-call | flops 240000008192 | bytes 60000000 | tf_op jit(solution)/shard_map/layer/pallas_call | solution.py:400
  223.2 0.5 broadcast.409
  223.8 1.4 reduce.3
  225.1 0.1 reshape.372
  225.2 0.1 copy.36
  225.3 0.7 slice.26
  226.0 0.1 reshape.370
  226.1 0.1 reshape.371
  226.2 0.1 copy.35
  226.3 0.8 reshape.368
  227.1 0.1 copy.33
  227.3 0.1 copy.38
  227.4 0.8 pad.9.clone
  228.2 46.2 %table.1 = (f32[2,128,25600]{2,1,0:T(8,128)}, bf16[16,512,512]{2,1,0:T(8,128)(2,1)}) custom-call(s32[16384]{0:T(1024)} %bitcast.38, f32[4,4096,128]{2,1,0:T(8,128)} %get-tuple-element.42.rows_hbm, bf16[16,512,512]{2,1,0:T(8,128)(2,1)} %get-tuple-element.43.lo_ref), custom_call_target="tpu_custom_call" | custom-call | flops 4000000000 | bytes 34000000 | tf_op jit(solution)/shard_map/table/pallas_call | solution.py:488
  274.4 96.0 %tail.1 = (f32[8,25152]{1,0:T(8,128)}, f32[8,3200]{1,0:T(8,128)}) custom-call(f32[2,4,4,8,25600]{4,3,2,1,0:T(8,128)} %bitcast.25, f32[4,4,4,8,6144]{4,3,2,1,0:T(8,128)} %bitcast.26, f32[2,4,4,4,8,128]{5,4,3,2,1,0:T(8,128)} %bitcast.29), custom_call_target="tpu_custom_call" | custom-call | tf_op jit(solution)/shard_map/tail/pallas_call | solution.py:700
  370.4 2.2 finish.1
  (10 shorter events, 0.1 us)
Async XLA Ops:
  0.6 8.0 %copy-start.1 = (bf16[512,1024]{1,0:T(8,128)(2,1)S(1)}, bf16[512,1024]{1,0:T(8,128)(2,1)}, u32[]{:S(2)}) copy-start(bf16[512,1024]{1,0:T(8,128)(2,1)} %fo_ref.1) | copy-start | bytes 3145732
  2.8 39.6 %collective-permute-start = (f32[4,1024]{1,0:T(4,128)}, f32[4,1024]{1,0:T(4,128)}, u32[]{:S(2)}, u32[]{:S(2)}) collective-permute-start(f32[4,1024]{1,0:T(4,128)} %fusion.15.bo_ref), channel_id=1, source_target_pairs={{0,64},{64,0},{1,65},{65,1},{2,66},{66,2},{3,67},{67,3},{4,68},{68... | collective-permute-start | bytes 49160 | tf_op jit(solution)/shard_map/ppermute | solution.py:743
  4.0 6.2 %copy-start = (bf16[3,4,64,512]{3,2,1,0:T(8,128)(2,1)}, bf16[3,4,64,512]{3,2,1,0:T(8,128)(2,1)S(1)}, u32[]{:S(2)}) copy-start(bf16[3,4,64,512]{3,2,1,0:T(8,128)(2,1)S(1)} %copy.32) | copy-start | bytes 2359300
  4.0 6.2 %copy-start.2 = (s32[16,512]{1,0:T(8,128)S(1)}, s32[16,512]{1,0:T(8,128)}, u32[]{:S(2)}) copy-start(s32[16,512]{1,0:T(8,128)} %param.15) | copy-start | bytes 98308
  8.2 34.2 %collective-permute-start.1 = (f32[2048,512]{1,0:T(8,128)}, f32[2048,512]{1,0:T(8,128)}, u32[]{:S(2)}, u32[]{:S(2)}) collective-permute-start(f32[2048,512]{1,0:T(8,128)} %maximum_convert_fusion), channel_id=1, source_target_pairs={{0,64},{64,0},{1,65},{65,1},{2,66},{66,2},{3,67},{67,3},{4,68},{68... | collective-permute-start | bytes 12582920 | tf_op jit(solution)/shard_map/ppermute | solution.py:743
  10.2 32.2 %collective-permute-start.2 = (f32[512,1024]{1,0:T(8,128)}, f32[512,1024]{1,0:T(8,128)}, u32[]{:S(2)}, u32[]{:S(2)}) collective-permute-start(f32[512,1024]{1,0:T(8,128)} %convert_element_type.38), channel_id=1, source_target_pairs={{0,64},{64,0},{1,65},{65,1},{2,66},{66,2},{3,67},{67,3},{4,68},{68... | collective-permute-start | bytes 6291464 | tf_op jit(solution)/shard_map/ppermute | solution.py:743
